TPU v7x, 32 devices: a 4x4x1 block of a 4x4x8 slice. The times are simulated.
32 devices in a mesh: pod: 1 (over z), data: 4 (over y), model: 8 (over x, core).
Axes of the slice: x: 4, y: 4, z: 1, core: 2. Of those that a mesh axis runs over, the one named last changes fastest.
The devices are a block of a 4x4x8 slice.
Arguments:
- x_in: bfloat16 [4, 512, 6144], P(('pod', 'data'), 'model')
- dy_in: bfloat16 [4, 512, 6144], P(('pod', 'data'), 'model')
- w_q: bfloat16 [6144, 48, 128], P(None, 'model')
- w_k: bfloat16 [4, 6144, 128], replicated
- w_v: bfloat16 [4, 6144, 128], replicated
- w_o: bfloat16 [48, 128, 6144], P('model')
Outputs:
- output 1: bfloat16 [4, 512, 6144], P(('pod', 'data'), 'model')
- output 2: float32 [6144, 48, 128], P(('pod', 'data'), 'model')
- output 3: float32 [24576, 128], P(('pod', 'model', 'data'))
- output 4: float32 [24576, 128], P(('pod', 'model', 'data'))
- output 5: float32 [48, 128, 6144], P(('pod', 'model'), None, 'data')
All inputs are finite; a program needn't handle non-finite values.
Results may differ from a plain program's by a relative error of at most 0.0094734.
Values are sent between devices in bfloat16 or wider.
A program may use at most 768 MiB of HBM per device.

v0:
```python
import jax
import jax.numpy as jnp
from jax import lax
from jax.sharding import PartitionSpec as P


def subgroup_pairs(step_shift, sub_size, axis_size):
    return [(start_dev + member, start_dev + (member + step_shift) % sub_size)
            for start_dev in range(0, axis_size, sub_size) for member in range(sub_size)]


def subgroup_scatter_sum(grad_parts, sub_size, axis_size):
    my_slot = lax.axis_index('model') % sub_size
    lead_dim, row_count, col_count = grad_parts.shape
    row_blocks = grad_parts.reshape(lead_dim, sub_size, row_count // sub_size, col_count)
    total_sum = lax.dynamic_index_in_dim(row_blocks, my_slot, axis=1, keepdims=False)
    for step_shift in range(1, sub_size):
        outgoing = lax.dynamic_index_in_dim(row_blocks, (my_slot + step_shift) % sub_size, axis=1, keepdims=False)
        total_sum = total_sum + lax.ppermute(outgoing, 'model', subgroup_pairs(step_shift, sub_size, axis_size))
    return total_sum


def solution(mesh):
    model_size = mesh.shape['model']
    tok_spec = P(('pod', 'data'), 'model', None)

    def device_step(x_loc, dy_loc, w_q, w_k, w_v, w_o):
        kv_heads = w_k.shape[0]
        head_dim = w_k.shape[2]
        sub_size = model_size // kv_heads
        score_scale = head_dim ** -0.5
        kv_index = lax.axis_index('model') // sub_size
        x_full = lax.all_gather(x_loc, 'model', axis=1, tiled=True)
        dy_full = lax.all_gather(dy_loc, 'model', axis=1, tiled=True)
        kv_weights = jnp.stack([lax.dynamic_index_in_dim(w_k, kv_index, axis=0, keepdims=False),
                                lax.dynamic_index_in_dim(w_v, kv_index, axis=0, keepdims=False)])
        seq_len = x_full.shape[1]
        causal = lax.broadcasted_iota(jnp.int32, (seq_len, seq_len), 0) >= lax.broadcasted_iota(jnp.int32, (seq_len, seq_len), 1)
        q_loc = jnp.einsum('btd,dhe->bhte', x_full, w_q, preferred_element_type=jnp.float32).astype(jnp.bfloat16)
        kv_loc = jnp.einsum('btd,nde->nbte', x_full, kv_weights, preferred_element_type=jnp.float32).astype(jnp.bfloat16)
        k_loc = kv_loc[0]
        v_loc = kv_loc[1]
        scores = jnp.einsum('bhqe,bke->bhqk', q_loc, k_loc, preferred_element_type=jnp.float32) * score_scale
        attn_prob = jax.nn.softmax(jnp.where(causal, scores, -jnp.inf), axis=-1)
        prob_bf = attn_prob.astype(jnp.bfloat16)
        out_loc = jnp.einsum('bhqk,bke->bhqe', prob_bf, v_loc, preferred_element_type=jnp.float32).astype(jnp.bfloat16)
        dout_loc = jnp.einsum('btd,hed->bhte', dy_full, w_o, preferred_element_type=jnp.float32).astype(jnp.bfloat16)
        grad_prob = jnp.einsum('bhqe,bke->bhqk', dout_loc, v_loc, preferred_element_type=jnp.float32)
        row_delta = jnp.einsum('bhqe,bhqe->bhq', dout_loc, out_loc, preferred_element_type=jnp.float32)
        grad_score = (attn_prob * (grad_prob - row_delta[..., None])).astype(jnp.bfloat16)
        grad_q = (jnp.einsum('bhqk,bke->bhqe', grad_score, k_loc, preferred_element_type=jnp.float32) * score_scale).astype(jnp.bfloat16)
        grad_k = jnp.einsum('bhqk,bhqe->bke', grad_score, q_loc, preferred_element_type=jnp.float32) * score_scale
        grad_v = jnp.einsum('bhqk,bhqe->bke', prob_bf, dout_loc, preferred_element_type=jnp.float32)
        grad_kv = jnp.stack([grad_k, grad_v]).astype(jnp.bfloat16)
        dx_part = (jnp.einsum('bhte,dhe->btd', grad_q, w_q, preferred_element_type=jnp.float32)
                   + jnp.einsum('nbte,nde->btd', grad_kv, kv_weights, preferred_element_type=jnp.float32))
        dwq_part = jnp.einsum('btd,bhte->dhe', x_full, grad_q, preferred_element_type=jnp.float32)
        dwkv_part = jnp.einsum('btd,nbte->nde', x_full, grad_kv, preferred_element_type=jnp.float32)
        dwo_part = jnp.einsum('bhte,btd->hed', out_loc, dy_full, preferred_element_type=jnp.float32)
        dx_loc = lax.psum_scatter(dx_part, 'model', scatter_dimension=1, tiled=True).astype(jnp.bfloat16)
        dwkv_sub = subgroup_scatter_sum(dwkv_part, sub_size, model_size)
        dwkv_loc = lax.psum_scatter(dwkv_sub, 'data', scatter_dimension=1, tiled=True)
        dwq_loc = lax.psum_scatter(dwq_part, 'data', scatter_dimension=0, tiled=True)
        dwo_loc = lax.psum_scatter(dwo_part, 'data', scatter_dimension=2, tiled=True)
        return dx_loc, dwq_loc, dwkv_loc[0], dwkv_loc[1], dwo_loc

    kv_rows = P(('pod', 'model', 'data'), None)
    return jax.shard_map(device_step, mesh=mesh,
                         in_specs=(tok_spec, tok_spec, P(None, 'model', None), P(), P(), P('model', None, None)),
                         out_specs=(tok_spec, P(('pod', 'data'), 'model', None), kv_rows, kv_rows, P(('pod', 'model'), None, 'data')),
                         check_vma=False)
```

profile of v0, /device:TPU:97, one launch (start us, length us, event | category | flops | bytes accessed | tf_op | source)
XLA Modules:
  0.0 610.7 jit_solution(2593674569636494617)
XLA Ops:
  8.9 3.2 constant_dynamic-slice_fusion.2
  12.8 2.3 copy.57
  16.0 35.9 %all-gather.5.cloned.1.call-done = bf16[1,512,6144]{2,1,0:T(8,128)(2,1)} async-done(((bf16[1,64,6144]{2,1,0:T(8,128)(2,1)}), bf16[1,512,6144]{2,1,0:T(8,128)(2,1)}) %all-gather.5.cloned.1.call-update) | async-done | bytes 6291472 | tf_op jit(solution)/shard_map/all_gather | solution.py:34
  52.0 10.7 %fusion.23 = bf16[6,512,128]{1,2,0:T(8,128)(2,1)} fusion(bf16[6,128,6144]{2,1,0:T(8,128)(2,1)} %param.11, bf16[1,512,6144]{2,1,0:T(8,128)(2,1)} %all-gather.5.cloned.1.call-done), kind=kOutput, calls=%fused_computation.31 | convolution fusion | flops 4832231424 | bytes 16515072 | tf_op jit(solution)/shard_map/btd,hed->bhte/dot_general | solution.py:47
  62.7 2.5 copy.43
  65.2 26.6 %all-gather.3.cloned.1.call-done = bf16[1,512,6144]{2,1,0:T(8,128)(2,1)} async-done(((bf16[1,64,6144]{2,1,0:T(8,128)(2,1)}), bf16[1,512,6144]{2,1,0:T(8,128)(2,1)}) %all-gather.3.cloned.1.call-update) | async-done | bytes 6291472 | tf_op jit(solution)/shard_map/all_gather | solution.py:33
  91.8 11.0 %fusion.26 = bf16[6,512,128]{1,2,0:T(8,128)(2,1)} fusion(bf16[6144,6,128]{2,0,1:T(8,128)(2,1)} %param.8, bf16[1,512,6144]{2,1,0:T(8,128)(2,1)} %all-gather.3.cloned.1.call-done), kind=kOutput, calls=%fused_computation.32 | convolution fusion | flops 4832231424 | bytes 16515072 | tf_op jit(solution)/shard_map/btd,dhe->bhte/dot_general | solution.py:39
  102.8 1.8 fusion.32
  104.7 6.2 %fusion.48 = (f32[6,512]{1,0:T(8,128)S(1)}, f32[6,512,512]{1,2,0:T(8,128)}) fusion(pred[512,512]{0,1:T(8,128)(4,1)} %iota_compare_fusion, bf16[6,512,128]{1,2,0:T(8,128)(2,1)} %fusion.26, bf16[2,1,512,128]{2,3,0,1:T(8,128)(2,1)S(1)} %fusion.32), kind=kOutput, calls=%fused_computation.59 | convolution fusion | flops 408945152 | bytes 7483392 | tf_op jit(solution)/shard_map/sub | solution.py:44
  110.8 3.9 fusion.16
  115.7 2.1 multiply_reduce_fusion
  117.9 1.6 multiply_convert_fusion
  119.5 1.7 copy-done.7
  122.2 4.5 convolution_bitcast_fusion.1
  126.7 9.1 %reshape.132 = f32[2,2,3072,128]{2,1,3,0:T(2,128)} reshape(f32[2,6144,128]{1,2,0:T(8,128)} %convolution_bitcast_fusion.1) | data formatting | bytes 12582912 | tf_op jit(solution)/shard_map/reshape | solution.py:15
  135.8 12.8 %constant_dynamic-slice_fusion.1 = (f32[2,1,3072,128]{2,1,3,0:T(1,128)S(1)}, f32[2,1,3072,128]{2,1,3,0:T(1,128)}) fusion(f32[2,2,3072,128]{2,1,3,0:T(2,128)} %reshape.132, s32[]{:T(128)S(6)} %select_n.36, s32[]{:T(128)S(6)} %select_n.38), kind=kLoop, calls=%fused_computation.51 | loop fusion | bytes 12582920 | tf_op jit(solution)/shard_map/jit(dynamic_index_in_dim)/dynamic_slice | solution.py:16
  148.6 7.6 %copy.29 = f32[2,1,3072,128]{3,2,0,1:T(8,128)} copy(f32[2,1,3072,128]{2,1,3,0:T(1,128)} %get-tuple-element.11) | data formatting | bytes 6291456 | tf_op jit(solution)/shard_map/jit(dynamic_index_in_dim)/dynamic_slice | solution.py:18
  156.5 5.1 copy.28
  161.9 5.0 bitcast_add_fusion.1
  167.0 2.8 multiply_convert_fusion.1
  169.8 8.0 %fusion.49 = f32[512,6144,1]{1,0,2:T(8,128)S(1)} fusion(bf16[6,512,128]{2,1,0:T(8,128)(2,1)} %multiply_convert_fusion.1, bf16[6144,6,128]{2,0,1:T(8,128)(2,1)} %param.8), kind=kOutput, calls=%fused_computation.60 | convolution fusion | flops 4831838208 | bytes 22806528 | tf_op jit(solution)/shard_map/bhte,dhe->btd/dot_general | solution.py:55
  177.8 6.9 %fusion.1 = f32[1,512,6144]{2,1,0:T(8,128)} fusion(f32[512,6144,1]{1,0,2:T(8,128)S(1)} %fusion.49, bf16[1,6144,128]{1,2,0:T(8,128)(2,1)} %copy-done.3, bf16[1,6144,128]{1,2,0:T(8,128)(2,1)S(1)} %copy-done.2, bf16[1,512,128]{2,1,0:T(8,128)(2,1)S(1)} %fusion.38, bf16[1,512,128]{2,1,0:T(8,128)(2,1)S(1)} %fusion.39), kind=kOutput, calls=%fused_computation.2 | convolution fusion | flops 1615462400 | bytes 28573696 | tf_op jit(solution)/shard_map/nbte,nde->btd/dot_general | solution.py:56
  184.9 1.0 copy-done.6
  185.9 12.2 %convolution_bitcast_fusion = f32[6144,6,128]{0,2,1:T(8,128)} fusion(bf16[6,512,128]{2,1,0:T(8,128)(2,1)S(1)} %copy-done.6, bf16[1,512,6144]{2,1,0:T(8,128)(2,1)} %all-gather.3.cloned.1.call-done), kind=kOutput, calls=%fused_computation.3 | convolution fusion | flops 4831838208 | bytes 25952256 | tf_op jit(solution)/shard_map/btd,bhte->dhe/dot_general | solution.py:57
  198.2 1.0 copy-done.5
  199.2 11.9 %fusion.2 = f32[6,128,6144]{2,1,0:T(8,128)} fusion(bf16[6,512,128]{2,1,0:T(8,128)(2,1)S(1)} %copy-done.5, bf16[1,512,6144]{2,1,0:T(8,128)(2,1)} %all-gather.5.cloned.1.call-done), kind=kOutput, calls=%fused_computation.5 | convolution fusion | flops 4831838208 | bytes 25952256 | tf_op jit(solution)/shard_map/bhte,btd->hed/dot_general | solution.py:59
  211.2 2.0 slice_bitcast_fusion
  213.2 60.7 %reduce-scatter.5.cloned.1.call-done = f32[1,64,6144]{2,1,0:T(8,128)} async-done(((f32[1,512,6144]{2,1,0:T(8,128)}), f32[1,64,6144]{2,1,0:T(8,128)}) %reduce-scatter.5.cloned.1.call-update) | async-done | bytes 1572880 | tf_op jit(solution)/shard_map/reduce_scatter | solution.py:60
  273.9 2.4 convert_element_type.64
  276.3 162.2 %reduce-scatter.7.cloned.1.call-done = f32[1536,6,128]{0,2,1:T(8,128)} async-done(((f32[6144,6,128]{0,2,1:T(8,128)}), f32[1536,6,128]{0,2,1:T(8,128)}) %reduce-scatter.7.cloned.1.call-update) | async-done | bytes 4718608 | tf_op jit(solution)/shard_map/reduce_scatter | solution.py:63
  438.5 6.0 copy.31
  444.5 158.9 %reduce-scatter.11.cloned.1.call-done = f32[6,128,1536]{2,1,0:T(8,128)} async-done(((f32[6,128,6144]{2,1,0:T(8,128)}), f32[6,128,1536]{2,1,0:T(8,128)}) %reduce-scatter.11.cloned.1.call-update) | async-done | bytes 4718608 | tf_op jit(solution)/shard_map/reduce_scatter | solution.py:64
  (50 shorter events, 6.2 us)
Async XLA Ops:
  7.2 44.8 %all-gather.5.cloned.1.call-start = ((), (), s32[]{:S(2)}) async-start(), calls=%async_computation.5 | async-start | bytes 7077888 | tf_op jit(solution)/shard_map/all_gather | solution.py:34
  8.0 83.8 %all-gather.3.cloned.1.call-start = ((), (), s32[]{:S(2)}) async-start(), calls=%async_computation.4 | async-start | bytes 7077888 | tf_op jit(solution)/shard_map/all_gather | solution.py:33
  8.8 202.4 %reduce-scatter.9.cloned.1.call-start = ((), (), s32[]{:S(2)}) async-start(), calls=%async_computation.8 | async-start | bytes 3932160 | tf_op jit(solution)/shard_map/reduce_scatter | solution.py:62
  12.8 90.0 %copy-start.1 = (bf16[1,6144,128]{1,2,0:T(8,128)(2,1)}, bf16[1,6144,128]{1,2,0:T(8,128)(2,1)S(1)}, u32[]{:S(2)}) copy-start(bf16[1,6144,128]{1,2,0:T(8,128)(2,1)S(1)} %copy.56) | copy-start | bytes 4718596
  15.1 87.7 %copy-start.3 = (bf16[1,6144,128]{1,2,0:T(8,128)(2,1)}, bf16[1,6144,128]{1,2,0:T(8,128)(2,1)S(1)}, u32[]{:S(2)}) copy-start(bf16[1,6144,128]{1,2,0:T(8,128)(2,1)S(1)} %copy.57) | copy-start | bytes 4718596
  91.8 11.0 %copy-start = (bf16[1,512,6144]{2,1,0:T(8,128)(2,1)S(1)}, bf16[1,512,6144]{2,1,0:T(8,128)(2,1)}, u32[]{:S(2)}) copy-start(bf16[1,512,6144]{2,1,0:T(8,128)(2,1)} %all-gather.3.cloned.1.call-done) | copy-start | bytes 18874372
  104.7 13.2 %copy-start.10 = (bf16[2,1,512,128]{2,3,0,1:T(8,128)(2,1)}, bf16[2,1,512,128]{2,3,0,1:T(8,128)(2,1)S(1)}, u32[]{:S(2)}) copy-start(bf16[2,1,512,128]{2,3,0,1:T(8,128)(2,1)S(1)} %fusion.32) | copy-start | bytes 786436
  110.8 3.9 copy-start.9
  110.8 4.9 copy-start.4
  110.8 7.1 %slice-start.2 = ((s8[6291456]{0:T(1024)(128)(4,1)}), s8[4194304]{0:T(1024)(128)(4,1)S(1)}, s32[]{:S(2)}) async-start(s8[6291456]{0:T(1024)(128)(4,1)} %bitcast.125), calls=%async_computation.12 | async-start | bytes 8388608
  114.7 3.2 slice-start.3
  115.7 6.4 %slice-start = ((s8[6291456]{0:T(1024)(128)(4,1)}), s8[4194304]{0:T(1024)(128)(4,1)S(1)}, s32[]{:S(2)}) async-start(s8[6291456]{0:T(1024)(128)(4,1)} %bitcast.123), calls=%async_computation.10 | async-start | bytes 8388608
  117.9 3.3 copy-start.11
  117.9 4.2 slice-start.1
  119.5 1.7 copy-start.7
  156.3 5.6 collective-permute-start
  161.6 5.4 copy-start.8
  166.9 107.0 %reduce-scatter.5.cloned.1.call-start = ((), (), s32[]{:S(2)}) async-start(), calls=%async_computation.6 | async-start | bytes 14155776 | tf_op jit(solution)/shard_map/reduce_scatter | solution.py:60
  169.8 8.0 %copy-start.2 = (bf16[1,6144,128]{1,2,0:T(8,128)(2,1)S(1)}, bf16[1,6144,128]{1,2,0:T(8,128)(2,1)}, u32[]{:S(2)}) copy-start(bf16[1,6144,128]{1,2,0:T(8,128)(2,1)} %copy-done.1) | copy-start | bytes 4718596
  184.7 1.1 copy-start.6
  184.8 253.7 %reduce-scatter.7.cloned.1.call-start = ((), (), s32[]{:S(2)}) async-start(), calls=%async_computation.7 | async-start | bytes 23592960 | tf_op jit(solution)/shard_map/reduce_scatter | solution.py:63
  198.0 1.1 copy-start.5
  198.1 405.3 %reduce-scatter.11.cloned.1.call-start = ((), (), s32[]{:S(2)}) async-start(), calls=%async_computation.9 | async-start | bytes 23592960 | tf_op jit(solution)/shard_map/reduce_scatter | solution.py:64
Sparse Core Ops, SparseCore 0:
  9.6 42.3 all-gather.4
  53.6 38.1 all-gather.2
  167.0 35.2 reduce-scatter.8
  204.5 69.3 reduce-scatter.4
  276.1 162.2 reduce-scatter.6
  441.3 162.0 reduce-scatter.10
where the time goes:
time: 617 us; the launch traced here: 611 us
  waiting for transfers between devices  446 us (72%)
  matrix products  81.6 us (13%)
  local copies, waits for them, and re-layouts  55.2 us (9%)
  between operations  14.9 us (2%)
  other arithmetic  12.1 us (2%)
    reduce_scatter x1, waiting for transfers between devices, device_step(): lax.psum_scatter(dwq_part, 'data', scatter_dimension=0, tiled=True)  162 us
    reduce_scatter x1, waiting for transfers between devices, device_step(): lax.psum_scatter(dwo_part, 'data', scatter_dimension=2, tiled=True)  159 us
    reduce_scatter x1, waiting for transfers between devices, device_step(): lax.psum_scatter(dx_part, 'model', scatter_dimension=1, tiled=True)  60.7 us
    all_gather x1, waiting for transfers between devices, device_step(): dy_full = lax.all_gather(dy_loc, 'model', axis=1, tiled=True)  35.9 us
    all_gather x1, waiting for transfers between devices, device_step(): x_full = lax.all_gather(x_loc, 'model', axis=1, tiled=True)  26.6 us
    dynamic_slice x2, local copies, waits for them, and re-layouts, subgroup_scatter_sum(): lax.dynamic_index_in_dim(row_blocks, my_slot, axis=1, keepdims=False)  17.9 us
    unnamed x36, local copies, waits for them, and re-layouts  15.3 us
  transfers between devices with their start and end apart: 7, of which 6 were waited for; matrix products, arithmetic and copies ran while one was open for 13% of the time, Pallas kernels for 0%

commit v1 on v0

v1 whole, which is shorter than its diff:
```python
import functools

import jax
import jax.numpy as jnp
from jax import lax
from jax.experimental import pallas as pl
from jax.experimental.pallas import tpu as pltpu
from jax.sharding import PartitionSpec as P

MESH = pl.DeviceIdType.MESH
F32 = jnp.float32
BF16 = jnp.bfloat16
VMEM_BYTES = 67043328


def dot(a, b, ca, cb):
    return lax.dot_general(a, b, (((ca,), (cb,)), ((), ())), preferred_element_type=F32)


def tile_of(n, t):
    return t if n % t == 0 else n


def kernel(cfg, x_ref, dy_ref, wq_ref, wk_ref, wv_ref, wo_ref,
           dx_ref, dwq_ref, dwk_ref, dwv_ref, dwo_ref,
           XS, DYS, XC, DYC, OA, DQA, QB, DOB, KV, QACC, KVACC, DKVR, DKVB,
           WQ, WKV, WO, MY, SX, RX, DXO, KS, KR, KOUT, OWQ, OWO,
           agr, ags, a2ar, a2as, yr, ys, dkr, dks, pxr, pxs, rsr, rss, exs, exr,
           lx, ldy, lwq, lwkv, lwo, lout):
    T, CW, E, NX, NY, NH = cfg
    NP = NH // 2
    R = 2 * NX * T
    HR = NX * T
    TH = T // 2
    scale = E ** -0.5
    pod = lax.axis_index('pod')
    y = lax.axis_index('data')
    m = lax.axis_index('model')
    c = lax.div(m, 2)
    h = lax.rem(m, 2)

    def at(dy_, dx_):
        return (pod, lax.rem(y + dy_ + NY, NY), 2 * lax.rem(c + dx_ + NX, NX) + h)

    XR, XL = at(0, 1), at(0, -1)
    YU, YD = at(1, 0), at(-1, 0)
    PT = (pod, y, 2 * c + 1 - h)

    def rc(src, dst, ssem, rsem, dev):
        return pltpu.make_async_remote_copy(src_ref=src, dst_ref=dst, send_sem=ssem, recv_sem=rsem,
                                            device_id=dev, device_id_type=MESH)

    def wait_recv(dst, sem):
        rc(dst, dst, sem, sem, PT).wait_recv()

    def wait_send(src, sem):
        rc(src, src, sem, sem, PT).wait_send()

    def chip(k):
        return lax.rem(c + k + NX, NX)

    def seq(k):
        return lax.rem(y + k + NY, NY)

    def rb(k):
        return pl.multiple_of((h * NX + chip(k)) * T, T)

    my_rows = rb(0)
    lxc = [pltpu.make_async_copy(x_ref.at[:, pl.ds(k * CW, CW)], XS.at[k, pl.ds(my_rows, T)], lx.at[k]) for k in range(NY)]
    ldc = [pltpu.make_async_copy(dy_ref.at[:, pl.ds(k * CW, CW)], DYS.at[k, pl.ds(my_rows, T)], ldy.at[k]) for k in range(NY)]
    for cp in lxc + ldc:
        cp.start()

    def wq_cp(k):
        return pltpu.make_async_copy(wq_ref.at[:, pl.ds(k * CW, CW), :], WQ, lwq.at[0])

    def wkv_cp(k):
        return [pltpu.make_async_copy(wk_ref.at[c, pl.ds(k * CW, CW)], WKV.at[0], lwkv.at[0]),
                pltpu.make_async_copy(wv_ref.at[c, pl.ds(k * CW, CW)], WKV.at[1], lwkv.at[1])]

    def wo_cp(k):
        return pltpu.make_async_copy(wo_ref.at[:, :, pl.ds(k * CW, CW)], WO, lwo.at[0])

    wq_cp(0).start()
    for cp in wkv_cp(0):
        cp.start()
    wo_cp(0).start()

    bar = pltpu.get_barrier_semaphore()
    peers = [XR, XL, PT] + [at(j, 0) for j in range(1, NY)]
    for dev in peers:
        pl.semaphore_signal(bar, inc=1, device_id=dev, device_id_type=MESH)
    pl.semaphore_wait(bar, len(peers))
    for cp in lxc + ldc:
        cp.wait()

    items = ([(XS, k) for k in range(NY)] + [(DYS, k) for k in range(NY)]
             + [(XC, seq(j)) for j in range(1, NY)] + [(DYC, seq(j)) for j in range(1, NY)])
    N_IT = len(items)

    def own(i):
        buf, ix = items[i]
        if i >= 2 * NY:
            t, j = divmod(i - 2 * NY, NY - 1)
            wait_recv(buf.at[ix, pl.ds(my_rows, T)], a2ar.at[t, j])
        blk = buf.at[ix, pl.ds(my_rows, T)]
        rc(blk, blk, ags.at[i], agr.at[i, 0], XR).start()
        rc(blk, blk, ags.at[i], agr.at[i, 1], XL).start()
        rc(blk, blk, ags.at[i], agr.at[i, 4], PT).start()

    def fwd(i):
        buf, ix = items[i]
        lb, rb_ = rb(-1), rb(1)
        blk = buf.at[ix, pl.ds(lb, T)]
        wait_recv(blk, agr.at[i, 0])
        half = buf.at[ix, pl.ds(lb, TH)]
        rc(half, half, ags.at[i], agr.at[i, 2], XR).start()
        rc(blk, blk, ags.at[i], agr.at[i, 4], PT).start()
        blk = buf.at[ix, pl.ds(rb_, T)]
        wait_recv(blk, agr.at[i, 1])
        half = buf.at[ix, pl.ds(pl.multiple_of(rb_ + TH, TH), TH)]
        rc(half, half, ags.at[i], agr.at[i, 3], XL).start()
        rc(blk, blk, ags.at[i], agr.at[i, 4], PT).start()

    def opp(i):
        buf, ix = items[i]
        ob = rb(2)
        wait_recv(buf.at[ix, pl.ds(ob, TH)], agr.at[i, 2])
        wait_recv(buf.at[ix, pl.ds(pl.multiple_of(ob + TH, TH), TH)], agr.at[i, 3])
        blk = buf.at[ix, pl.ds(ob, T)]
        rc(blk, blk, ags.at[i], agr.at[i, 4], PT).start()

    def fin(i):
        buf, ix = items[i]
        wait_recv(buf.at[ix, pl.ds(pl.multiple_of((1 - h) * HR, HR), HR)], agr.at[i, 4])

    def ag_sent(i):
        buf, ix = items[i]
        wait_send(buf.at[ix, pl.ds(0, 7 * T)], ags.at[i])

    def ybuf(q):
        return (OA if q < NP else DQA).at[q % NP]

    def yown(q):
        b = ybuf(q).at[y]
        rc(b, b, ys.at[q], yr.at[q, 0], YU).start()
        rc(b, b, ys.at[q], yr.at[q, 1], YD).start()

    def yfwd(q):
        b = ybuf(q)
        wait_recv(b.at[seq(-1)], yr.at[q, 0])
        half = b.at[seq(-1), pl.ds(0, HR)]
        rc(half, half, ys.at[q], yr.at[q, 2], YU).start()
        wait_recv(b.at[seq(1)], yr.at[q, 1])
        half = b.at[seq(1), pl.ds(HR, HR)]
        rc(half, half, ys.at[q], yr.at[q, 3], YD).start()

    def yopp(q):
        b = ybuf(q)
        wait_recv(b.at[seq(2), pl.ds(0, HR)], yr.at[q, 2])
        wait_recv(b.at[seq(2), pl.ds(HR, HR)], yr.at[q, 3])

    def ysent(q):
        wait_send(ybuf(q).at[pl.ds(0, 3)], ys.at[q])

    def proj_x(k):
        wq_cp(k).wait()
        for cp in wkv_cp(k):
            cp.wait()

        def body(p, _):
            w = jnp.concatenate([WQ[2 * p], WQ[2 * p + 1]], axis=1)
            d = dot(XS[k], w, 1, 0)
            QACC[p] = d if k == 0 else QACC[p] + d
            return 0
        lax.fori_loop(0, NP, body, 0)
        d = dot(XS[k], jnp.concatenate([WKV[0], WKV[1]], axis=1), 1, 0)
        KVACC[...] = d if k == 0 else KVACC[...] + d
        nk = (k + 1) % NY
        wq_cp(nk).start()
        for cp in wkv_cp(nk):
            cp.start()

    def proj_dy(k):
        wo_cp(k).wait()

        def body(p, _):
            w = WO[pl.ds(2 * p, 2)].reshape(2 * E, CW)
            d = dot(DYS[k], w, 1, 1)
            QACC[p] = d if k == 0 else QACC[p] + d
            return 0
        lax.fori_loop(0, NP, body, 0)
        if k + 1 < NY:
            wo_cp(k + 1).start()

    def copy_acc(dst):
        def body(p, _):
            dst[p] = QACC[p].astype(BF16)
            return 0
        lax.fori_loop(0, NP, body, 0)

    QR = HR

    def pos(i):
        g = lax.div(i, T)
        return (2 * lax.rem(g, NX) + lax.div(g, NX)) * T + lax.rem(i, T)

    def probs(p, a, rows0):
        q = QB[p, pl.ds(rows0, QR), a * E:(a + 1) * E]
        s = dot(q, KV[0], 1, 1) * scale
        qp = pos(lax.broadcasted_iota(jnp.int32, (QR, 1), 0) + rows0)
        kp = pos(lax.broadcasted_iota(jnp.int32, (1, R), 1))
        s = jnp.where(qp >= kp, s, -jnp.inf)
        e = jnp.exp(s - jnp.max(s, axis=1, keepdims=True))
        return q, e / jnp.sum(e, axis=1, keepdims=True)

    def attn_fwd(p):
        def body(b, _):
            rows0 = pl.multiple_of(b * QR, QR)
            for a in range(2):
                _, pr = probs(p, a, rows0)
                OA[p, y, pl.ds(rows0, QR), a * E:(a + 1) * E] = dot(pr.astype(BF16), KV[1], 1, 0).astype(BF16)
            return 0
        lax.fori_loop(0, R // QR, body, 0)

    def attn_bwd(p):
        def body(b, _):
            rows0 = pl.multiple_of(b * QR, QR)
            for a in range(2):
                ln = slice(a * E, (a + 1) * E)
                q, pr = probs(p, a, rows0)
                do = DOB[p, pl.ds(rows0, QR), ln]
                o = OA[p, y, pl.ds(rows0, QR), ln]
                delta = jnp.sum(do.astype(F32) * o.astype(F32), axis=1, keepdims=True)
                dp = dot(do, KV[1], 1, 1)
                ds = (pr * (dp - delta)).astype(BF16)
                DQA[p, y, pl.ds(rows0, QR), ln] = (dot(ds, KV[0], 1, 0) * scale).astype(BF16)
                KVACC[:, :E] = KVACC[:, :E] + dot(ds, q, 0, 0)
                KVACC[:, E:] = KVACC[:, E:] + dot(pr.astype(BF16), do, 0, 0)
            return 0
        lax.fori_loop(0, R // QR, body, 0)

    def dkv_send():
        KVACC[:, :E] = KVACC[:, :E] * scale
        rc(KVACC, DKVR, exs.at[0], exr.at[0], PT).start()

    def dkv_sum():
        wait_recv(DKVR, exr.at[0])
        tot = (KVACC[...] + DKVR[...]).astype(BF16)
        DKVB[0] = tot[:, :E]
        DKVB[1] = tot[:, E:]

    KB = CW // 2
    KT = tile_of(KB, 256)

    def dwkv_tile(r, t):
        ck = 2 * h + lax.div(r, 2)
        off = pl.multiple_of(KB * lax.rem(r, 2) + t * KT, KT)
        kv = jnp.concatenate([DKVB[0], DKVB[1]], axis=1)
        return dot(XS[ck, :, pl.ds(off, KT)], kv, 0, 0)

    def dwkv_send(j):
        r = seq(j)

        def body(t, _):
            KS[j - 1, pl.ds(pl.multiple_of(t * KT, KT), KT), :] = dwkv_tile(r, t).astype(BF16)
            return 0
        lax.fori_loop(0, KB // KT, body, 0)
        rc(KS.at[j - 1], KR.at[NY - j - 1], dks.at[0], dkr.at[NY - j - 1], at(j, 0)).start()

    def dwkv_final():
        for j in range(NY - 1):
            wait_recv(KR.at[j], dkr.at[j])

        def body(t, _):
            rows = pl.ds(pl.multiple_of(t * KT, KT), KT)
            v = dwkv_tile(y, t)
            for j in range(NY - 1):
                v = v + KR[j, rows, :].astype(F32)
            KOUT[0, rows, :] = v[:, :E]
            KOUT[1, rows, :] = v[:, E:]
            return 0
        lax.fori_loop(0, KB // KT, body, 0)
        for i, ref in enumerate((dwk_ref, dwv_ref)):
            pltpu.make_async_copy(KOUT.at[i], ref, lout.at[i]).start()

    def dwkv_out_wait():
        for i, ref in enumerate((dwk_ref, dwv_ref)):
            pltpu.make_async_copy(KOUT.at[i], ref, lout.at[i]).wait()

    NT = tile_of(CW, 256)

    def dxc(k):
        wq_cp(k).wait()
        for cp in wkv_cp(k):
            cp.wait()

        def body(t, _):
            off = pl.multiple_of(t * NT, NT)
            rows = pl.ds(off, NT)
            v = dot(DKVB[h], WKV[h, rows, :], 1, 1)
            for p in range(NP):
                w = jnp.concatenate([WQ[2 * p, rows, :], WQ[2 * p + 1, rows, :]], axis=1)
                v = v + dot(DQA[p, y], w, 1, 1)
            lo, hi = v[:HR], v[HR:]
            MY[k, :, pl.ds(off, NT)] = jnp.where(h == 0, lo, hi)
            DYS[k, pl.ds(HR, HR), pl.ds(off, NT)] = jnp.where(h == 0, hi, lo).astype(BF16)
            return 0
        lax.fori_loop(0, CW // NT, body, 0)
        if k + 1 < NY:
            wq_cp(k + 1).start()
            for cp in wkv_cp(k + 1):
                cp.start()
        rc(DYS.at[k, pl.ds(HR, HR)], DYS.at[k, pl.ds(0, HR)], pxs.at[k], pxr.at[k], PT).start()

    def blk(k, cc, o, n):
        rows = pl.ds(pl.multiple_of(cc * T + o, TH), n)
        return MY[k, rows, :] + DYS[k, rows, :].astype(F32)

    def rs1(k):
        wait_recv(DYS.at[k, pl.ds(0, HR)], pxr.at[k])
        SX[k, 0:T, :] = blk(k, chip(2), 0, T).astype(BF16)
        s, d = SX.at[k, pl.ds(0, TH)], RX.at[k, pl.ds(0, TH)]
        rc(s, d, rss.at[k], rsr.at[k, 0], XR).start()
        s, d = SX.at[k, pl.ds(TH, TH)], RX.at[k, pl.ds(TH, TH)]
        rc(s, d, rss.at[k], rsr.at[k, 1], XL).start()

    def rs2(k):
        wait_recv(RX.at[k, pl.ds(0, TH)], rsr.at[k, 0])
        SX[k, T:T + TH, :] = (blk(k, chip(1), 0, TH) + RX[k, 0:TH, :].astype(F32)).astype(BF16)
        SX[k, T + TH:2 * T, :] = blk(k, chip(1), TH, TH).astype(BF16)
        s, d = SX.at[k, pl.ds(T, T)], RX.at[k, pl.ds(T, T)]
        rc(s, d, rss.at[k], rsr.at[k, 2], XR).start()
        wait_recv(RX.at[k, pl.ds(TH, TH)], rsr.at[k, 1])
        SX[k, 2 * T:2 * T + TH, :] = blk(k, chip(-1), 0, TH).astype(BF16)
        SX[k, 2 * T + TH:3 * T, :] = (blk(k, chip(-1), TH, TH) + RX[k, TH:T, :].astype(F32)).astype(BF16)
        s, d = SX.at[k, pl.ds(2 * T, T)], RX.at[k, pl.ds(2 * T, T)]
        rc(s, d, rss.at[k], rsr.at[k, 3], XL).start()

    def dx_out(k):
        return pltpu.make_async_copy(DXO.at[k], dx_ref.at[:, pl.ds(k * CW, CW)], lout.at[2 + k])

    def rs3(k):
        wait_recv(RX.at[k, pl.ds(T, T)], rsr.at[k, 2])
        wait_recv(RX.at[k, pl.ds(2 * T, T)], rsr.at[k, 3])
        v = blk(k, c, 0, T) + RX[k, T:2 * T, :].astype(F32) + RX[k, 2 * T:3 * T, :].astype(F32)
        DXO[k] = v.astype(BF16)
        dx_out(k).start()

    def dwo_out(p):
        return pltpu.make_async_copy(OWO, dwo_ref.at[pl.ds(2 * p, 2)], lout.at[2 + NY])

    def dwq_out(p):
        return pltpu.make_async_copy(OWQ, dwq_ref.at[pl.ds(2 * p, 2)], lout.at[3 + NY])

    OT = tile_of(CW, 512)

    def dwo(p):
        yopp(p)
        if p:
            dwo_out(p - 1).wait()

        def body(t, _):
            cols = pl.ds(pl.multiple_of(t * OT, OT), OT)
            v = dot(OA[p, 0], DYC[0, :, cols], 0, 0)
            for s in range(1, NY):
                v = v + dot(OA[p, s], DYC[s, :, cols], 0, 0)
            OWO[0, :, cols] = v[:E]
            OWO[1, :, cols] = v[E:]
            return 0
        lax.fori_loop(0, CW // OT, body, 0)
        dwo_out(p).start()

    def dwq(p):
        yopp(NP + p)
        if p:
            dwq_out(p - 1).wait()

        def body(t, _):
            cols = pl.ds(pl.multiple_of(t * NT, NT), NT)
            v = dot(XC[0, :, cols], DQA[p, 0], 0, 0)
            for s in range(1, NY):
                v = v + dot(XC[s, :, cols], DQA[p, s], 0, 0)
            OWQ[0, cols, :] = v[:, :E]
            OWQ[1, cols, :] = v[:, E:]
            return 0
        lax.fori_loop(0, CW // NT, body, 0)
        dwq_out(p).start()

    def own_cols(dst, src):
        def body(t, _):
            rows = pl.ds(pl.multiple_of(t * T, T), T)
            dst[y, rows, :] = src[y, rows, :]
            return 0
        lax.fori_loop(0, R // T, body, 0)

    own(0)
    own(1)
    for t, (src, dst) in enumerate(((XS, XC), (DYS, DYC))):
        for j in range(1, NY):
            rc(src.at[seq(j), pl.ds(my_rows, T)], dst.at[y, pl.ds(my_rows, T)],
               a2as.at[t], a2ar.at[t, NY - j - 1], at(j, 0)).start()

    def compute(i):
        if i < NY:
            proj_x(i)
            if i == NY - 1:
                copy_acc(QB)
                KV[0] = KVACC[:, :E].astype(BF16)
                KV[1] = KVACC[:, E:].astype(BF16)
                for p in range(NP):
                    attn_fwd(p)
                    yown(p)
                own_cols(XC, XS)
        elif i < 2 * NY:
            proj_dy(i - NY)
            if i >= NY + 1:
                yfwd(i - NY - 1)
            if i == 2 * NY - 1:
                copy_acc(DOB)
                own_cols(DYC, DYS)
                KVACC[...] = jnp.zeros_like(KVACC)
                attn_bwd(0)
                yown(NP)
        elif i < 2 * NY + NP - 1:
            p = i - 2 * NY + 1
            attn_bwd(p)
            yown(NP + p)
            if p == NP - 1:
                for k in range(NY):
                    ag_sent(NY + k)
                wait_send(DYS.at[0, pl.ds(0, 3 * T)], a2as.at[1])
                dkv_send()
        elif i == 2 * NY + NP - 1:
            dkv_sum()
            for j in range(1, NY):
                dwkv_send(j)
            yfwd(NP)
        elif i == 2 * NY + NP:
            dxc(0)
            yfwd(NP + 1)
        elif i == 2 * NY + NP + 1:
            dxc(1)
            rs1(0)
            yfwd(NP + 2)

    for i in range(N_IT + 1):
        if i < N_IT:
            fwd(i)
        if i + 2 < N_IT:
            own(i + 2)
        if i >= 1:
            opp(i - 1)
            fin(i - 1)
            compute(i - 1)

    rs1(1)
    rs2(0)
    dxc(2)
    rs1(2)
    rs2(1)
    dxc(3)
    rs1(3)
    rs2(2)
    rs3(0)
    dwo(0)
    rs2(3)
    rs3(1)
    dwq(0)
    rs3(2)
    dwo(1)
    dwq(1)
    rs3(3)
    dwo(2)
    dwq(2)
    dwkv_final()

    for i in list(range(NY)) + list(range(2 * NY, N_IT)):
        ag_sent(i)
    wait_send(XS.at[0, pl.ds(0, 3 * T)], a2as.at[0])
    for q in range(2 * NP):
        ysent(q)
    wait_send(KVACC, exs.at[0])
    wait_send(KS, dks.at[0])
    for k in range(NY):
        wait_send(DYS.at[k, pl.ds(HR, HR)], pxs.at[k])
        wait_send(SX.at[k], rss.at[k])
        dx_out(k).wait()
    dwkv_out_wait()
    dwo_out(NP - 1).wait()
    dwq_out(NP - 1).wait()


def solution(mesh):
    model_size = mesh.shape['model']
    tok_spec = P(('pod', 'data'), 'model', None)

    def device_step(x_loc, dy_loc, w_q, w_k, w_v, w_o):
        T, D = x_loc.shape[1:]
        NH, E = w_q.shape[1:]
        KVH = w_k.shape[0]
        NX = model_size // 2
        NY = mesh.shape['data']
        assert NX == 4 and NY == 4 and KVH == NX and NH == 6
        NP = NH // 2
        CW = D // NY
        R = model_size * T
        KB = CW // 2
        cfg = (T, CW, E, NX, NY, NH)
        V = pltpu.VMEM
        S = pltpu.SemaphoreType.DMA
        n_it = 4 * NY - 2
        scratch = [
            V((NY, R, CW), BF16), V((NY, R, CW), BF16), V((NY, R, CW), BF16), V((NY, R, CW), BF16),
            V((NP, NY, R, 2 * E), BF16), V((NP, NY, R, 2 * E), BF16),
            V((NP, R, 2 * E), BF16), V((NP, R, 2 * E), BF16), V((2, R, E), BF16),
            V((NP, R, 2 * E), F32), V((R, 2 * E), F32), V((R, 2 * E), F32), V((2, R, E), BF16),
            V((NH, CW, E), BF16), V((2, CW, E), BF16), V((NH, E, CW), BF16),
            V((NY, R // 2, CW), F32), V((NY, 3 * T, CW), BF16), V((NY, 3 * T, CW), BF16), V((NY, T, CW), BF16),
            V((NY - 1, KB, 2 * E), BF16), V((NY - 1, KB, 2 * E), BF16), V((2, KB, E), F32),
            V((2, CW, E), F32), V((2, E, CW), F32),
            S((n_it, 5)), S((n_it,)), S((2, NY - 1)), S((2,)), S((2 * NP, 4)), S((2 * NP,)),
            S((NY - 1,)), S((1,)), S((NY,)), S((NY,)), S((NY, 4)), S((NY,)), S((1,)), S((1,)),
            S((NY,)), S((NY,)), S((1,)), S((2,)), S((1,)), S((4 + NY,)),
        ]
        any_spec = pl.BlockSpec(memory_space=pl.ANY)
        dx, dwq, dwk, dwv, dwo = pl.pallas_call(
            functools.partial(kernel, cfg),
            out_shape=[jax.ShapeDtypeStruct((T, D), BF16), jax.ShapeDtypeStruct((NH, CW, E), F32),
                       jax.ShapeDtypeStruct((KB, E), F32), jax.ShapeDtypeStruct((KB, E), F32),
                       jax.ShapeDtypeStruct((NH, E, CW), F32)],
            in_specs=[any_spec] * 6,
            out_specs=[any_spec] * 5,
            scratch_shapes=scratch,
            compiler_params=pltpu.CompilerParams(collective_id=0, has_side_effects=True, vmem_limit_bytes=VMEM_BYTES),
            name='attn_bwd_fused',
        )(x_loc[0], dy_loc[0], w_q.transpose(1, 0, 2), w_k, w_v, w_o)
        return dx[None], dwq.transpose(1, 0, 2), dwk, dwv, dwo

    kv_rows = P(('pod', 'model', 'data'), None)
    return jax.shard_map(device_step, mesh=mesh,
                         in_specs=(tok_spec, tok_spec, P(None, 'model', None), P(), P(), P('model', None, None)),
                         out_specs=(tok_spec, P(('pod', 'data'), 'model', None), kv_rows, kv_rows, P(('pod', 'model'), None, 'data')),
                         check_vma=False)
```

time: 617 us -> 152 us (0.25)
  waiting for transfers between devices: 446 us -> 0 us
  Pallas kernels: 0 us -> 140 us
  matrix products: 81.6 us -> 0 us
  local copies, waits for them, and re-layouts: 55.2 us -> 10.8 us
  between operations: 14.9 us -> 0.67 us
  other arithmetic: 12.1 us -> 0.01 us
    reduce_scatter x4 -> x0, waiting for transfers between devices: 382 us -> none  [the longest x1 162 us: device_step(): lax.psum_scatter(dwq_part, 'data', scatter_dimension=0, tiled=True)]
    pallas_call x0 -> x1, Pallas kernels: none -> 140 us  [device_step(): pl.pallas_call(functools.partial(kernel, cfg), out_shape=[jax.ShapeDtypeS...]
    dot_general x13 -> x0, matrix products: 75.5 us -> none  [the longest x1 12.2 us: device_step(): jnp.einsum('btd,bhte->dhe', x_full, grad_q, preferred_element_type=jnp.fl...]
    all_gather x2 -> x0, waiting for transfers between devices: 62.5 us -> none  [the longest x1 35.9 us: device_step(): dy_full = lax.all_gather(dy_loc, 'model', axis=1, tiled=True)]
    dynamic_slice x4 -> x0, local copies, waits for them, and re-layouts: 28.7 us -> none  [the longest x2 17.9 us: subgroup_scatter_sum(): lax.dynamic_index_in_dim(row_blocks, my_slot, axis=1, keepdims=False)]
    reshape x1 -> x0, local copies, waits for them, and re-layouts: 9.14 us -> none  [subgroup_scatter_sum(): grad_parts.reshape(lead_dim, sub_size, row_count // sub_size, col_count)]
    convert_element_type x2 -> x0, other arithmetic: 6.23 us -> none  [the longest x1 3.87 us: device_step(): prob_bf = attn_prob.astype(jnp.bfloat16)]
    unnamed x36 -> x13, local copies, waits for them, and re-layouts: 15.3 us -> 10.8 us
  transfers between devices with their start and end apart: 7 -> 0, of which waited for: 6 -> 0; matrix products, arithmetic and copies ran while one was open for 13% -> 0% of each run, Pallas kernels for 0% -> 0%
where the time goes in v1:
time: 152 us
  Pallas kernels  140 us (92%)
  local copies, waits for them, and re-layouts  10.8 us (7%)
    pallas_call x1, Pallas kernels, device_step(): pl.pallas_call(functools.partial(kernel, cfg), out_shape=[jax.ShapeDtypeS...  140 us
    unnamed x13, local copies, waits for them, and re-layouts  10.8 us

profile of v1, /device:TPU:97, one launch (start us, length us, event | category | flops | bytes accessed | tf_op | source)
XLA Modules:
  0.0 151.6 jit_solution(1420330790056605599)
XLA Ops:
  0.6 140.2 %attn_bwd_fused.1 = (bf16[64,6144]{1,0:T(8,128)(2,1)}, f32[6,1536,128]{2,1,0:T(8,128)}, f32[768,128]{1,0:T(8,128)}, f32[768,128]{1,0:T(8,128)}, f32[6,128,1536]{2,1,0:T(8,128)}) custom-call(bf16[64,6144]{1,0:T(8,128)(2,1)} %bitcast.10, bf16[64,6144]{1,0:T(8,128)(2,1)} %bitcast.11, bf16[6,6144,128]{2,1,0:T(8,128)(2,1)} %bitcast.5, ...), custom_call_target="tpu_custom_call" | custom-call | tf_op jit(solution)/shard_map/attn_bwd_fused/pallas_call | solution.py:527
  140.8 0.0 copy-start.1
  140.8 0.0 copy-start
  140.8 0.0 slice-start
  140.8 2.2 %copy.16 = bf16[1,64,6144]{2,1,0:T(8,128)(2,1)} copy(bf16[1,64,6144]{2,1,0:T(8,128)(2,1)} %bitcast.9) | data formatting | bytes 1572864
  143.0 0.0 slice-start.1
  143.0 4.9 %copy.17 = f32[1536,6,128]{2,0,1:T(8,128)} copy(f32[1536,6,128]{2,0,1:T(8,128)} %bitcast.8) | data formatting | bytes 9437184
  147.9 0.0 copy-done.1
  147.9 0.7 copy.18
  148.7 0.0 copy-done
  148.7 0.7 copy.19
  149.4 0.0 slice-done
  149.4 0.0 slice-done.1
  149.4 2.2 %copy.20 = f32[6,128,1536]{2,1,0:T(8,128)} copy(f32[6,128,1536]{2,1,0:T(8,128)S(1)} %bitcast.7) | data formatting | bytes 9437184
  (1 shorter events, 0.0 us)
Async XLA Ops:
  140.8 7.1 %copy-start.1 = (f32[768,128]{1,0:T(8,128)S(1)}, f32[768,128]{1,0:T(8,128)}, u32[]{:S(2)}) copy-start(f32[768,128]{1,0:T(8,128)} %get-tuple-element.22) | copy-start | bytes 1179652
  140.8 7.9 %copy-start = (f32[768,128]{1,0:T(8,128)S(1)}, f32[768,128]{1,0:T(8,128)}, u32[]{:S(2)}) copy-start(f32[768,128]{1,0:T(8,128)} %get-tuple-element.23) | copy-start | bytes 1179652
  140.8 8.6 %slice-start = ((s8[4718592]{0:T(1024)(128)(4,1)}), s8[4194304]{0:T(1024)(128)(4,1)S(1)}, s32[]{:S(2)}) async-start(s8[4718592]{0:T(1024)(128)(4,1)} %bitcast.6), calls=%async_computation | async-start | bytes 8388608
  143.0 6.4 %slice-start.1 = ((s8[4718592]{0:T(1024)(128)(4,1)}), s8[524288]{0:T(1024)(128)(4,1)S(1)}, s32[]{:S(2)}) async-start(s8[4718592]{0:T(1024)(128)(4,1)} %bitcast.6), calls=%async_computation.1 | async-start | bytes 1048576

commit v2 on v1

--- a/solution.py
+++ b/solution.py
@@ -25,7 +25,7 @@
            dx_ref, dwq_ref, dwk_ref, dwv_ref, dwo_ref,
            XS, DYS, XC, DYC, OA, DQA, QB, DOB, KV, QACC, KVACC, DKVR, DKVB,
            WQ, WKV, WO, MY, SX, RX, DXO, KS, KR, KOUT, OWQ, OWO,
-           agr, ags, a2ar, a2as, yr, ys, dkr, dks, pxr, pxs, rsr, rss, exs, exr,
+           agr, ags, a2ar, a2as, xcr, xcs, yr, ys, dkr, dks, pxr, pxs, rsr, rss, exs, exr,
            lx, ldy, lwq, lwkv, lwo, lout):
     T, CW, E, NX, NY, NH = cfg
     NP = NH // 2
@@ -66,43 +66,46 @@
         return pl.multiple_of((h * NX + chip(k)) * T, T)
 
     my_rows = rb(0)
-    lxc = [pltpu.make_async_copy(x_ref.at[:, pl.ds(k * CW, CW)], XS.at[k, pl.ds(my_rows, T)], lx.at[k]) for k in range(NY)]
-    ldc = [pltpu.make_async_copy(dy_ref.at[:, pl.ds(k * CW, CW)], DYS.at[k, pl.ds(my_rows, T)], ldy.at[k]) for k in range(NY)]
-    for cp in lxc + ldc:
-        cp.start()
+    def mul(k, n):
+        return pl.multiple_of(k * n, n)
 
     def wq_cp(k):
-        return pltpu.make_async_copy(wq_ref.at[:, pl.ds(k * CW, CW), :], WQ, lwq.at[0])
+        return pltpu.make_async_copy(wq_ref.at[:, pl.ds(mul(k, CW), CW), :], WQ, lwq.at[0])
 
     def wkv_cp(k):
-        return [pltpu.make_async_copy(wk_ref.at[c, pl.ds(k * CW, CW)], WKV.at[0], lwkv.at[0]),
-                pltpu.make_async_copy(wv_ref.at[c, pl.ds(k * CW, CW)], WKV.at[1], lwkv.at[1])]
+        return [pltpu.make_async_copy(wk_ref.at[c, pl.ds(mul(k, CW), CW)], WKV.at[0], lwkv.at[0]),
+                pltpu.make_async_copy(wv_ref.at[c, pl.ds(mul(k, CW), CW)], WKV.at[1], lwkv.at[1])]
 
     def wo_cp(k):
         return pltpu.make_async_copy(wo_ref.at[:, :, pl.ds(k * CW, CW)], WO, lwo.at[0])
-
-    wq_cp(0).start()
-    for cp in wkv_cp(0):
-        cp.start()
-    wo_cp(0).start()
 
     bar = pltpu.get_barrier_semaphore()
     peers = [XR, XL, PT] + [at(j, 0) for j in range(1, NY)]
     for dev in peers:
         pl.semaphore_signal(bar, inc=1, device_id=dev, device_id_type=MESH)
+    x_order = [seq(1), seq(-1), seq(2), y]
+    lxc = [pltpu.make_async_copy(x_ref.at[:, pl.ds(k * CW, CW)], XS.at[k, pl.ds(my_rows, T)], lx.at[k]) for k in range(NY)]
+    ldc = [pltpu.make_async_copy(dy_ref.at[:, pl.ds(k * CW, CW)], DYS.at[k, pl.ds(my_rows, T)], ldy.at[k]) for k in range(NY)]
+    for cp in lxc:
+        cp.start()
+    for cp in lxc:
+        cp.wait()
+    for cp in ldc:
+        cp.start()
+    wq_cp(x_order[0]).start()
+    for cp in wkv_cp(x_order[0]):
+        cp.start()
+    wo_cp(0).start()
     pl.semaphore_wait(bar, len(peers))
-    for cp in lxc + ldc:
-        cp.wait()
-
-    items = ([(XS, k) for k in range(NY)] + [(DYS, k) for k in range(NY)]
-             + [(XC, seq(j)) for j in range(1, NY)] + [(DYC, seq(j)) for j in range(1, NY)])
+
+    items = ([(XS, k) for k in x_order] + [(DYS, k) for k in range(NY)]
+             + [(DYC, seq(j)) for j in range(1, NY)] + [(XC, seq(2))])
     N_IT = len(items)
 
     def own(i):
         buf, ix = items[i]
         if i >= 2 * NY:
-            t, j = divmod(i - 2 * NY, NY - 1)
-            wait_recv(buf.at[ix, pl.ds(my_rows, T)], a2ar.at[t, j])
+            wait_recv(buf.at[ix, pl.ds(my_rows, T)], a2ar.at[i - 2 * NY])
         blk = buf.at[ix, pl.ds(my_rows, T)]
         rc(blk, blk, ags.at[i], agr.at[i, 0], XR).start()
         rc(blk, blk, ags.at[i], agr.at[i, 1], XL).start()
@@ -138,6 +141,19 @@
         buf, ix = items[i]
         wait_send(buf.at[ix, pl.ds(0, 7 * T)], ags.at[i])
 
+    par = pl.ds(mul(h, HR), HR)
+
+    def xc_send(n):
+        rc(XS.at[x_order[n], par], XC.at[y, par], xcs.at[n], xcr.at[n], (YU, YD)[n]).start()
+
+    def xc_fwd(n):
+        b = XC.at[seq((-1, 1)[n]), par]
+        wait_recv(b, xcr.at[n])
+        rc(b, b, xcs.at[2 + n], xcr.at[2 + n], PT).start()
+
+    def xc_fin(n):
+        wait_recv(XC.at[seq((-1, 1)[n]), pl.ds(mul(1 - h, HR), HR)], xcr.at[2 + n])
+
     def ybuf(q):
         return (OA if q < NP else DQA).at[q % NP]
 
@@ -163,7 +179,8 @@
     def ysent(q):
         wait_send(ybuf(q).at[pl.ds(0, 3)], ys.at[q])
 
-    def proj_x(k):
+    def proj_x(i):
+        k = x_order[i]
         wq_cp(k).wait()
         for cp in wkv_cp(k):
             cp.wait()
@@ -171,12 +188,12 @@
         def body(p, _):
             w = jnp.concatenate([WQ[2 * p], WQ[2 * p + 1]], axis=1)
             d = dot(XS[k], w, 1, 0)
-            QACC[p] = d if k == 0 else QACC[p] + d
+            QACC[p] = d if i == 0 else QACC[p] + d
             return 0
         lax.fori_loop(0, NP, body, 0)
         d = dot(XS[k], jnp.concatenate([WKV[0], WKV[1]], axis=1), 1, 0)
-        KVACC[...] = d if k == 0 else KVACC[...] + d
-        nk = (k + 1) % NY
+        KVACC[...] = d if i == 0 else KVACC[...] + d
+        nk = x_order[i + 1] if i + 1 < NY else 0
         wq_cp(nk).start()
         for cp in wkv_cp(nk):
             cp.start()
@@ -259,24 +276,35 @@
         kv = jnp.concatenate([DKVB[0], DKVB[1]], axis=1)
         return dot(XS[ck, :, pl.ds(off, KT)], kv, 0, 0)
 
-    def dwkv_send(j):
-        r = seq(j)
-
+    KH = KB // 2
+
+    def dwkv_early():
         def body(t, _):
-            KS[j - 1, pl.ds(pl.multiple_of(t * KT, KT), KT), :] = dwkv_tile(r, t).astype(BF16)
+            KS[0, pl.ds(mul(t, KT), KT), :] = dwkv_tile(seq(2), t).astype(BF16)
             return 0
         lax.fori_loop(0, KB // KT, body, 0)
-        rc(KS.at[j - 1], KR.at[NY - j - 1], dks.at[0], dkr.at[NY - j - 1], at(j, 0)).start()
+        rc(KS.at[0, pl.ds(0, KH)], KR.at[0, pl.ds(0, KH)], dks.at[0], dkr.at[0], YU).start()
+        rc(KS.at[0, pl.ds(KH, KH)], KR.at[0, pl.ds(KH, KH)], dks.at[0], dkr.at[1], YD).start()
+
+    def dwkv_mid():
+        for n, (j, dev) in enumerate(((1, YU), (-1, YD))):
+            def body(t, _):
+                KS[n + 1, pl.ds(mul(t, KT), KT), :] = dwkv_tile(seq(j), t).astype(BF16)
+                return 0
+            lax.fori_loop(0, KB // KT, body, 0)
+        for n, (j, dev) in enumerate(((1, YU), (-1, YD))):
+            half = pl.ds(n * KH, KH)
+            wait_recv(KR.at[0, half], dkr.at[n])
+            KS[n + 1, half, :] = (KS[n + 1, half, :].astype(F32) + KR[0, half, :].astype(F32)).astype(BF16)
+            rc(KS.at[n + 1], KR.at[n + 1], dks.at[n + 1], dkr.at[n + 2], dev).start()
 
     def dwkv_final():
-        for j in range(NY - 1):
-            wait_recv(KR.at[j], dkr.at[j])
+        for n in range(2):
+            wait_recv(KR.at[n + 1], dkr.at[n + 2])
 
         def body(t, _):
-            rows = pl.ds(pl.multiple_of(t * KT, KT), KT)
-            v = dwkv_tile(y, t)
-            for j in range(NY - 1):
-                v = v + KR[j, rows, :].astype(F32)
+            rows = pl.ds(mul(t, KT), KT)
+            v = dwkv_tile(y, t) + KR[1, rows, :].astype(F32) + KR[2, rows, :].astype(F32)
             KOUT[0, rows, :] = v[:, :E]
             KOUT[1, rows, :] = v[:, E:]
             return 0
@@ -396,15 +424,19 @@
 
     own(0)
     own(1)
-    for t, (src, dst) in enumerate(((XS, XC), (DYS, DYC))):
-        for j in range(1, NY):
-            rc(src.at[seq(j), pl.ds(my_rows, T)], dst.at[y, pl.ds(my_rows, T)],
-               a2as.at[t], a2ar.at[t, NY - j - 1], at(j, 0)).start()
+    rc(XS.at[seq(2), pl.ds(my_rows, T)], XC.at[y, pl.ds(my_rows, T)], a2as.at[0], a2ar.at[3], at(2, 0)).start()
+    for cp in ldc:
+        cp.wait()
+    for j in range(1, NY):
+        rc(DYS.at[seq(j), pl.ds(my_rows, T)], DYC.at[y, pl.ds(my_rows, T)],
+           a2as.at[1], a2ar.at[NY - j - 1], at(j, 0)).start()
 
     def compute(i):
         if i < NY:
+            if i < 2:
+                xc_send(i)
             proj_x(i)
-            if i == NY - 1:
+            if i == 3:
                 copy_acc(QB)
                 KV[0] = KVACC[:, :E].astype(BF16)
                 KV[1] = KVACC[:, E:].astype(BF16)
@@ -412,37 +444,41 @@
                     attn_fwd(p)
                     yown(p)
                 own_cols(XC, XS)
-        elif i < 2 * NY:
+        elif i < 8:
             proj_dy(i - NY)
-            if i >= NY + 1:
-                yfwd(i - NY - 1)
-            if i == 2 * NY - 1:
+            if i == 5:
+                xc_fwd(0)
+            if i == 6:
+                xc_fwd(1)
+                yfwd(0)
+            if i == 7:
                 copy_acc(DOB)
                 own_cols(DYC, DYS)
                 KVACC[...] = jnp.zeros_like(KVACC)
                 attn_bwd(0)
                 yown(NP)
-        elif i < 2 * NY + NP - 1:
-            p = i - 2 * NY + 1
-            attn_bwd(p)
-            yown(NP + p)
-            if p == NP - 1:
-                for k in range(NY):
-                    ag_sent(NY + k)
-                wait_send(DYS.at[0, pl.ds(0, 3 * T)], a2as.at[1])
-                dkv_send()
-        elif i == 2 * NY + NP - 1:
+                yfwd(1)
+        elif i == 8:
+            attn_bwd(1)
+            yown(NP + 1)
+            attn_bwd(2)
+            yown(NP + 2)
+            for k in range(NY):
+                ag_sent(NY + k)
+            wait_send(DYS.at[0, pl.ds(0, 3 * T)], a2as.at[1])
+            dkv_send()
+            yfwd(2)
+        elif i == 9:
             dkv_sum()
-            for j in range(1, NY):
-                dwkv_send(j)
+            dxc(0)
+            dwkv_early()
+            dxc(1)
+        elif i == 10:
+            dxc(2)
+            rs1(0)
+            dxc(3)
+            rs1(1)
             yfwd(NP)
-        elif i == 2 * NY + NP:
-            dxc(0)
-            yfwd(NP + 1)
-        elif i == 2 * NY + NP + 1:
-            dxc(1)
-            rs1(0)
-            yfwd(NP + 2)
 
     for i in range(N_IT + 1):
         if i < N_IT:
@@ -451,37 +487,46 @@
             own(i + 2)
         if i >= 1:
             opp(i - 1)
-            fin(i - 1)
+            if i - 1 < 2 * NY:
+                fin(i - 1)
             compute(i - 1)
 
-    rs1(1)
+    rs1(2)
+    rs1(3)
+    yfwd(NP + 1)
+    dwkv_mid()
+    yfwd(NP + 2)
+    for i in range(2 * NY, 2 * NY + 3):
+        fin(i)
     rs2(0)
-    dxc(2)
-    rs1(2)
+    dwo(0)
     rs2(1)
-    dxc(3)
-    rs1(3)
+    dwo(1)
     rs2(2)
+    dwo(2)
+    rs2(3)
+    xc_fin(0)
+    xc_fin(1)
+    fin(N_IT - 1)
+    dwq(0)
     rs3(0)
-    dwo(0)
-    rs2(3)
+    dwq(1)
     rs3(1)
-    dwq(0)
+    dwq(2)
     rs3(2)
-    dwo(1)
-    dwq(1)
+    dwkv_final()
     rs3(3)
-    dwo(2)
-    dwq(2)
-    dwkv_final()
 
     for i in list(range(NY)) + list(range(2 * NY, N_IT)):
         ag_sent(i)
-    wait_send(XS.at[0, pl.ds(0, 3 * T)], a2as.at[0])
+    wait_send(XS.at[0, pl.ds(0, T)], a2as.at[0])
+    for n in range(4):
+        wait_send(XC.at[0, par], xcs.at[n])
     for q in range(2 * NP):
         ysent(q)
     wait_send(KVACC, exs.at[0])
-    wait_send(KS, dks.at[0])
+    for n in range(3):
+        wait_send(KS.at[n], dks.at[n])
     for k in range(NY):
         wait_send(DYS.at[k, pl.ds(HR, HR)], pxs.at[k])
         wait_send(SX.at[k], rss.at[k])
@@ -509,7 +554,7 @@
         cfg = (T, CW, E, NX, NY, NH)
         V = pltpu.VMEM
         S = pltpu.SemaphoreType.DMA
-        n_it = 4 * NY - 2
+        n_it = 3 * NY
         scratch = [
             V((NY, R, CW), BF16), V((NY, R, CW), BF16), V((NY, R, CW), BF16), V((NY, R, CW), BF16),
             V((NP, NY, R, 2 * E), BF16), V((NP, NY, R, 2 * E), BF16),
@@ -519,8 +564,8 @@
             V((NY, R // 2, CW), F32), V((NY, 3 * T, CW), BF16), V((NY, 3 * T, CW), BF16), V((NY, T, CW), BF16),
             V((NY - 1, KB, 2 * E), BF16), V((NY - 1, KB, 2 * E), BF16), V((2, KB, E), F32),
             V((2, CW, E), F32), V((2, E, CW), F32),
-            S((n_it, 5)), S((n_it,)), S((2, NY - 1)), S((2,)), S((2 * NP, 4)), S((2 * NP,)),
-            S((NY - 1,)), S((1,)), S((NY,)), S((NY,)), S((NY, 4)), S((NY,)), S((1,)), S((1,)),
+            S((n_it, 5)), S((n_it,)), S((NY,)), S((2,)), S((4,)), S((4,)), S((2 * NP, 4)), S((2 * NP,)),
+            S((4,)), S((3,)), S((NY,)), S((NY,)), S((NY, 4)), S((NY,)), S((1,)), S((1,)),
             S((NY,)), S((NY,)), S((1,)), S((2,)), S((1,)), S((4 + NY,)),
         ]
         any_spec = pl.BlockSpec(memory_space=pl.ANY)

time: 152 us -> 137 us (0.901)
  Pallas kernels: 140 us -> 125 us
    pallas_call x1, Pallas kernels: 140 us -> 125 us  [device_step(): pl.pallas_call(functools.partial(kernel, cfg), out_shape=[jax.ShapeDtypeS...]
where the time goes in v2:
time: 137 us; the launch traced here: 136 us
  Pallas kernels  125 us (91%)
  local copies, waits for them, and re-layouts  10.8 us (8%)
    pallas_call x1, Pallas kernels, device_step(): pl.pallas_call(functools.partial(kernel, cfg), out_shape=[jax.ShapeDtypeS...  125 us
    unnamed x13, local copies, waits for them, and re-layouts  10.8 us

profile of v2, /device:TPU:97, one launch (start us, length us, event | category | flops | bytes accessed | tf_op | source)
XLA Modules:
  0.0 136.0 jit_solution(14449665254242547206)
XLA Ops:
  0.6 124.5 %attn_bwd_fused.1 = (bf16[64,6144]{1,0:T(8,128)(2,1)}, f32[6,1536,128]{2,1,0:T(8,128)}, f32[768,128]{1,0:T(8,128)}, f32[768,128]{1,0:T(8,128)}, f32[6,128,1536]{2,1,0:T(8,128)}) custom-call(bf16[64,6144]{1,0:T(8,128)(2,1)} %bitcast.10, bf16[64,6144]{1,0:T(8,128)(2,1)} %bitcast.11, bf16[6,6144,128]{2,1,0:T(8,128)(2,1)} %bitcast.5, ...), custom_call_target="tpu_custom_call" | custom-call | tf_op jit(solution)/shard_map/attn_bwd_fused/pallas_call | solution.py:572
  125.1 0.0 copy-start.1
  125.2 0.0 copy-start
  125.2 0.0 slice-start
  125.2 2.2 %copy.16 = bf16[1,64,6144]{2,1,0:T(8,128)(2,1)} copy(bf16[1,64,6144]{2,1,0:T(8,128)(2,1)} %bitcast.9) | data formatting | bytes 1572864
  127.4 0.0 slice-start.1
  127.4 4.9 %copy.17 = f32[1536,6,128]{2,0,1:T(8,128)} copy(f32[1536,6,128]{2,0,1:T(8,128)} %bitcast.8) | data formatting | bytes 9437184
  132.3 0.0 copy-done.1
  132.3 0.7 copy.18
  133.0 0.0 copy-done
  133.0 0.7 copy.19
  133.8 0.0 slice-done
  133.8 0.0 slice-done.1
  133.8 2.2 %copy.20 = f32[6,128,1536]{2,1,0:T(8,128)} copy(f32[6,128,1536]{2,1,0:T(8,128)S(1)} %bitcast.7) | data formatting | bytes 9437184
  (1 shorter events, 0.0 us)
Async XLA Ops:
  125.1 7.1 %copy-start.1 = (f32[768,128]{1,0:T(8,128)S(1)}, f32[768,128]{1,0:T(8,128)}, u32[]{:S(2)}) copy-start(f32[768,128]{1,0:T(8,128)} %get-tuple-element.22) | copy-start | bytes 1179652
  125.2 7.9 %copy-start = (f32[768,128]{1,0:T(8,128)S(1)}, f32[768,128]{1,0:T(8,128)}, u32[]{:S(2)}) copy-start(f32[768,128]{1,0:T(8,128)} %get-tuple-element.23) | copy-start | bytes 1179652
  125.2 8.6 %slice-start = ((s8[4718592]{0:T(1024)(128)(4,1)}), s8[4194304]{0:T(1024)(128)(4,1)S(1)}, s32[]{:S(2)}) async-start(s8[4718592]{0:T(1024)(128)(4,1)} %bitcast.6), calls=%async_computation | async-start | bytes 8388608
  127.4 6.4 %slice-start.1 = ((s8[4718592]{0:T(1024)(128)(4,1)}), s8[524288]{0:T(1024)(128)(4,1)S(1)}, s32[]{:S(2)}) async-start(s8[4718592]{0:T(1024)(128)(4,1)} %bitcast.6), calls=%async_computation.1 | async-start | bytes 1048576

commit v3 on v2

--- a/solution.py
+++ b/solution.py
@@ -10,7 +10,8 @@
 MESH = pl.DeviceIdType.MESH
 F32 = jnp.float32
 BF16 = jnp.bfloat16
-VMEM_BYTES = 67043328
+VMEM_BYTES = 54 * 1000 * 1000
+LOG2E = 1.4426950408889634
 
 
 def dot(a, b, ca, cb):
@@ -23,16 +24,17 @@
 
 def kernel(cfg, x_ref, dy_ref, wq_ref, wk_ref, wv_ref, wo_ref,
            dx_ref, dwq_ref, dwk_ref, dwv_ref, dwo_ref,
-           XS, DYS, XC, DYC, OA, DQA, QB, DOB, KV, QACC, KVACC, DKVR, DKVB,
-           WQ, WKV, WO, MY, SX, RX, DXO, KS, KR, KOUT, OWQ, OWO,
+           XS, DYS, XC, DYC, OA, DQA, QB, DOB, KV, KVACC, DKVR, DKVB,
+           WQ, WKV, WO, MY, KS, KR,
            agr, ags, a2ar, a2as, xcr, xcs, yr, ys, dkr, dks, pxr, pxs, rsr, rss, exs, exr,
-           lx, ldy, lwq, lwkv, lwo, lout):
+           lx, ldy, lwq, lwkv, lwo, cred):
     T, CW, E, NX, NY, NH = cfg
     NP = NH // 2
     R = 2 * NX * T
     HR = NX * T
     TH = T // 2
     scale = E ** -0.5
+    scale2 = scale * LOG2E
     pod = lax.axis_index('pod')
     y = lax.axis_index('data')
     m = lax.axis_index('model')
@@ -179,6 +181,11 @@
     def ysent(q):
         wait_send(ybuf(q).at[pl.ds(0, 3)], ys.at[q])
 
+    def acc(p, d, first):
+        cols = pl.ds(mul(p, 2 * E), 2 * E)
+        MY[0, :, cols] = d[:HR] if first else MY[0, :, cols] + d[:HR]
+        MY[1, :, cols] = d[HR:] if first else MY[1, :, cols] + d[HR:]
+
     def proj_x(i):
         k = x_order[i]
         wq_cp(k).wait()
@@ -187,8 +194,7 @@
 
         def body(p, _):
             w = jnp.concatenate([WQ[2 * p], WQ[2 * p + 1]], axis=1)
-            d = dot(XS[k], w, 1, 0)
-            QACC[p] = d if i == 0 else QACC[p] + d
+            acc(p, dot(XS[k], w, 1, 0), i == 0)
             return 0
         lax.fori_loop(0, NP, body, 0)
         d = dot(XS[k], jnp.concatenate([WKV[0], WKV[1]], axis=1), 1, 0)
@@ -203,8 +209,7 @@
 
         def body(p, _):
             w = WO[pl.ds(2 * p, 2)].reshape(2 * E, CW)
-            d = dot(DYS[k], w, 1, 1)
-            QACC[p] = d if k == 0 else QACC[p] + d
+            acc(p, dot(DYS[k], w, 1, 1), k == 0)
             return 0
         lax.fori_loop(0, NP, body, 0)
         if k + 1 < NY:
@@ -212,50 +217,75 @@
 
     def copy_acc(dst):
         def body(p, _):
-            dst[p] = QACC[p].astype(BF16)
+            cols = pl.ds(mul(p, 2 * E), 2 * E)
+            dst[p, 0:HR, :] = MY[0, :, cols].astype(BF16)
+            dst[p, HR:R, :] = MY[1, :, cols].astype(BF16)
             return 0
         lax.fori_loop(0, NP, body, 0)
 
-    QR = HR
+    T2 = 2 * T
 
     def pos(i):
         g = lax.div(i, T)
         return (2 * lax.rem(g, NX) + lax.div(g, NX)) * T + lax.rem(i, T)
 
-    def probs(p, a, rows0):
-        q = QB[p, pl.ds(rows0, QR), a * E:(a + 1) * E]
-        s = dot(q, KV[0], 1, 1) * scale
-        qp = pos(lax.broadcasted_iota(jnp.int32, (QR, 1), 0) + rows0)
-        kp = pos(lax.broadcasted_iota(jnp.int32, (1, R), 1))
+    def brow(i, g):
+        return lax.div(i, T2) * HR + g * T2 + lax.rem(i, T2)
+
+    def pick(load, g):
+        return jnp.concatenate([load(slice(g * T2, g * T2 + T2)), load(slice(HR + g * T2, HR + g * T2 + T2))], axis=0)
+
+    def put(store, g, v):
+        store(slice(g * T2, g * T2 + T2), v[:T2])
+        store(slice(HR + g * T2, HR + g * T2 + T2), v[T2:])
+
+    def keys(t, g):
+        return pick(lambda r: KV[t, r, :], 0) if g == 0 else KV[t]
+
+    def probs(q, g):
+        s = dot(q, keys(0, g), 1, 1) * scale2
+        n = s.shape[1]
+        qp = pos(brow(lax.broadcasted_iota(jnp.int32, (HR, 1), 0), g))
+        kp = lax.broadcasted_iota(jnp.int32, (1, n), 1)
+        kp = pos(brow(kp, 0) if g == 0 else kp)
         s = jnp.where(qp >= kp, s, -jnp.inf)
-        e = jnp.exp(s - jnp.max(s, axis=1, keepdims=True))
-        return q, e / jnp.sum(e, axis=1, keepdims=True)
+        e = jnp.exp2(s - jnp.max(s, axis=1, keepdims=True))
+        return e * (1.0 / jnp.sum(e, axis=1, keepdims=True))
 
     def attn_fwd(p):
-        def body(b, _):
-            rows0 = pl.multiple_of(b * QR, QR)
-            for a in range(2):
-                _, pr = probs(p, a, rows0)
-                OA[p, y, pl.ds(rows0, QR), a * E:(a + 1) * E] = dot(pr.astype(BF16), KV[1], 1, 0).astype(BF16)
-            return 0
-        lax.fori_loop(0, R // QR, body, 0)
-
-    def attn_bwd(p):
-        def body(b, _):
-            rows0 = pl.multiple_of(b * QR, QR)
+        for g in range(2):
             for a in range(2):
                 ln = slice(a * E, (a + 1) * E)
-                q, pr = probs(p, a, rows0)
-                do = DOB[p, pl.ds(rows0, QR), ln]
-                o = OA[p, y, pl.ds(rows0, QR), ln]
+                pr = probs(pick(lambda r: QB[p, r, ln], g), g)
+                o = dot(pr.astype(BF16), keys(1, g), 1, 0).astype(BF16)
+
+                def store(r, v):
+                    OA[p, y, r, ln] = v
+                put(store, g, o)
+
+    def attn_bwd(p):
+        for g in range(2):
+            for a in range(2):
+                ln = slice(a * E, (a + 1) * E)
+                q = pick(lambda r: QB[p, r, ln], g)
+                do = pick(lambda r: DOB[p, r, ln], g)
+                o = pick(lambda r: OA[p, y, r, ln], g)
+                pr = probs(q, g)
                 delta = jnp.sum(do.astype(F32) * o.astype(F32), axis=1, keepdims=True)
-                dp = dot(do, KV[1], 1, 1)
+                dp = dot(do, keys(1, g), 1, 1)
                 ds = (pr * (dp - delta)).astype(BF16)
-                DQA[p, y, pl.ds(rows0, QR), ln] = (dot(ds, KV[0], 1, 0) * scale).astype(BF16)
-                KVACC[:, :E] = KVACC[:, :E] + dot(ds, q, 0, 0)
-                KVACC[:, E:] = KVACC[:, E:] + dot(pr.astype(BF16), do, 0, 0)
-            return 0
-        lax.fori_loop(0, R // QR, body, 0)
+                dq = (dot(ds, keys(0, g), 1, 0) * scale).astype(BF16)
+                dkv = jnp.concatenate([dot(ds, q, 0, 0), dot(pr.astype(BF16), do, 0, 0)], axis=1)
+
+                def store(r, v):
+                    DQA[p, y, r, ln] = v
+                put(store, g, dq)
+                if g == 0:
+                    def add(r, v):
+                        KVACC[r, :] = KVACC[r, :] + v
+                    put(add, 0, dkv)
+                else:
+                    KVACC[...] = KVACC[...] + dkv
 
     def dkv_send():
         KVACC[:, :E] = KVACC[:, :E] * scale
@@ -286,13 +316,23 @@
         rc(KS.at[0, pl.ds(0, KH)], KR.at[0, pl.ds(0, KH)], dks.at[0], dkr.at[0], YU).start()
         rc(KS.at[0, pl.ds(KH, KH)], KR.at[0, pl.ds(KH, KH)], dks.at[0], dkr.at[1], YD).start()
 
+    def dwkv_part(n):
+        def body(t, _):
+            KS[n + 1, pl.ds(mul(t, KT), KT), :] = dwkv_tile(seq((1, -1)[n]), t).astype(BF16)
+            return 0
+        lax.fori_loop(0, KB // KT, body, 0)
+
+    def dwkv_own():
+        def body(t, _):
+            rows = pl.ds(mul(t, KT), KT)
+            v = dwkv_tile(y, t)
+            dwk_ref[rows, :] = v[:, :E]
+            dwv_ref[rows, :] = v[:, E:]
+            return 0
+        lax.fori_loop(0, KB // KT, body, 0)
+
     def dwkv_mid():
-        for n, (j, dev) in enumerate(((1, YU), (-1, YD))):
-            def body(t, _):
-                KS[n + 1, pl.ds(mul(t, KT), KT), :] = dwkv_tile(seq(j), t).astype(BF16)
-                return 0
-            lax.fori_loop(0, KB // KT, body, 0)
-        for n, (j, dev) in enumerate(((1, YU), (-1, YD))):
+        for n, dev in enumerate((YU, YD)):
             half = pl.ds(n * KH, KH)
             wait_recv(KR.at[0, half], dkr.at[n])
             KS[n + 1, half, :] = (KS[n + 1, half, :].astype(F32) + KR[0, half, :].astype(F32)).astype(BF16)
@@ -304,17 +344,20 @@
 
         def body(t, _):
             rows = pl.ds(mul(t, KT), KT)
-            v = dwkv_tile(y, t) + KR[1, rows, :].astype(F32) + KR[2, rows, :].astype(F32)
-            KOUT[0, rows, :] = v[:, :E]
-            KOUT[1, rows, :] = v[:, E:]
+            v = KR[1, rows, :].astype(F32) + KR[2, rows, :].astype(F32)
+            dwk_ref[rows, :] = dwk_ref[rows, :] + v[:, :E]
+            dwv_ref[rows, :] = dwv_ref[rows, :] + v[:, E:]
             return 0
         lax.fori_loop(0, KB // KT, body, 0)
-        for i, ref in enumerate((dwk_ref, dwv_ref)):
-            pltpu.make_async_copy(KOUT.at[i], ref, lout.at[i]).start()
-
-    def dwkv_out_wait():
-        for i, ref in enumerate((dwk_ref, dwv_ref)):
-            pltpu.make_async_copy(KOUT.at[i], ref, lout.at[i]).wait()
+
+    def x_free():
+        for i in range(NY):
+            ag_sent(i)
+        wait_send(XS.at[0, pl.ds(0, T)], a2as.at[0])
+        for n in range(2):
+            wait_send(XS.at[0, par], xcs.at[n])
+        for dev in (XL, XR):
+            pl.semaphore_signal(cred, inc=1, device_id=dev, device_id_type=MESH)
 
     NT = tile_of(CW, 256)
 
@@ -326,10 +369,8 @@
         def body(t, _):
             off = pl.multiple_of(t * NT, NT)
             rows = pl.ds(off, NT)
-            v = dot(DKVB[h], WKV[h, rows, :], 1, 1)
-            for p in range(NP):
-                w = jnp.concatenate([WQ[2 * p, rows, :], WQ[2 * p + 1, rows, :]], axis=1)
-                v = v + dot(DQA[p, y], w, 1, 1)
+            w = jnp.concatenate([WQ[i, rows, :] for i in range(NH)] + [WKV[h, rows, :]], axis=1)
+            v = dot(jnp.concatenate([DQA[p, y] for p in range(NP)] + [DKVB[h]], axis=1), w, 1, 1)
             lo, hi = v[:HR], v[HR:]
             MY[k, :, pl.ds(off, NT)] = jnp.where(h == 0, lo, hi)
             DYS[k, pl.ds(HR, HR), pl.ds(off, NT)] = jnp.where(h == 0, hi, lo).astype(BF16)
@@ -341,79 +382,57 @@
                 cp.start()
         rc(DYS.at[k, pl.ds(HR, HR)], DYS.at[k, pl.ds(0, HR)], pxs.at[k], pxr.at[k], PT).start()
 
+    RO = 3 * T
+
     def blk(k, cc, o, n):
         rows = pl.ds(pl.multiple_of(cc * T + o, TH), n)
         return MY[k, rows, :] + DYS[k, rows, :].astype(F32)
 
     def rs1(k):
         wait_recv(DYS.at[k, pl.ds(0, HR)], pxr.at[k])
-        SX[k, 0:T, :] = blk(k, chip(2), 0, T).astype(BF16)
-        s, d = SX.at[k, pl.ds(0, TH)], RX.at[k, pl.ds(0, TH)]
+        XS[k, 0:T, :] = blk(k, chip(2), 0, T).astype(BF16)
+        s, d = XS.at[k, pl.ds(0, TH)], XS.at[k, pl.ds(RO + 0, TH)]
         rc(s, d, rss.at[k], rsr.at[k, 0], XR).start()
-        s, d = SX.at[k, pl.ds(TH, TH)], RX.at[k, pl.ds(TH, TH)]
+        s, d = XS.at[k, pl.ds(TH, TH)], XS.at[k, pl.ds(RO + TH, TH)]
         rc(s, d, rss.at[k], rsr.at[k, 1], XL).start()
 
     def rs2(k):
-        wait_recv(RX.at[k, pl.ds(0, TH)], rsr.at[k, 0])
-        SX[k, T:T + TH, :] = (blk(k, chip(1), 0, TH) + RX[k, 0:TH, :].astype(F32)).astype(BF16)
-        SX[k, T + TH:2 * T, :] = blk(k, chip(1), TH, TH).astype(BF16)
-        s, d = SX.at[k, pl.ds(T, T)], RX.at[k, pl.ds(T, T)]
+        wait_recv(XS.at[k, pl.ds(RO + 0, TH)], rsr.at[k, 0])
+        XS[k, T:T + TH, :] = (blk(k, chip(1), 0, TH) + XS[k, RO + 0:RO + TH, :].astype(F32)).astype(BF16)
+        XS[k, T + TH:2 * T, :] = blk(k, chip(1), TH, TH).astype(BF16)
+        s, d = XS.at[k, pl.ds(T, T)], XS.at[k, pl.ds(RO + T, T)]
         rc(s, d, rss.at[k], rsr.at[k, 2], XR).start()
-        wait_recv(RX.at[k, pl.ds(TH, TH)], rsr.at[k, 1])
-        SX[k, 2 * T:2 * T + TH, :] = blk(k, chip(-1), 0, TH).astype(BF16)
-        SX[k, 2 * T + TH:3 * T, :] = (blk(k, chip(-1), TH, TH) + RX[k, TH:T, :].astype(F32)).astype(BF16)
-        s, d = SX.at[k, pl.ds(2 * T, T)], RX.at[k, pl.ds(2 * T, T)]
+        wait_recv(XS.at[k, pl.ds(RO + TH, TH)], rsr.at[k, 1])
+        XS[k, 2 * T:2 * T + TH, :] = blk(k, chip(-1), 0, TH).astype(BF16)
+        XS[k, 2 * T + TH:3 * T, :] = (blk(k, chip(-1), TH, TH) + XS[k, RO + TH:RO + T, :].astype(F32)).astype(BF16)
+        s, d = XS.at[k, pl.ds(2 * T, T)], XS.at[k, pl.ds(RO + 2 * T, T)]
         rc(s, d, rss.at[k], rsr.at[k, 3], XL).start()
 
-    def dx_out(k):
-        return pltpu.make_async_copy(DXO.at[k], dx_ref.at[:, pl.ds(k * CW, CW)], lout.at[2 + k])
-
     def rs3(k):
-        wait_recv(RX.at[k, pl.ds(T, T)], rsr.at[k, 2])
-        wait_recv(RX.at[k, pl.ds(2 * T, T)], rsr.at[k, 3])
-        v = blk(k, c, 0, T) + RX[k, T:2 * T, :].astype(F32) + RX[k, 2 * T:3 * T, :].astype(F32)
-        DXO[k] = v.astype(BF16)
-        dx_out(k).start()
-
-    def dwo_out(p):
-        return pltpu.make_async_copy(OWO, dwo_ref.at[pl.ds(2 * p, 2)], lout.at[2 + NY])
-
-    def dwq_out(p):
-        return pltpu.make_async_copy(OWQ, dwq_ref.at[pl.ds(2 * p, 2)], lout.at[3 + NY])
+        wait_recv(XS.at[k, pl.ds(RO + T, T)], rsr.at[k, 2])
+        wait_recv(XS.at[k, pl.ds(RO + 2 * T, T)], rsr.at[k, 3])
+        v = blk(k, c, 0, T) + XS[k, RO + T:RO + 2 * T, :].astype(F32) + XS[k, RO + 2 * T:RO + 3 * T, :].astype(F32)
+        dx_ref[:, k * CW:(k + 1) * CW] = v.astype(BF16)
 
     OT = tile_of(CW, 512)
 
     def dwo(p):
-        yopp(p)
-        if p:
-            dwo_out(p - 1).wait()
-
-        def body(t, _):
-            cols = pl.ds(pl.multiple_of(t * OT, OT), OT)
-            v = dot(OA[p, 0], DYC[0, :, cols], 0, 0)
-            for s in range(1, NY):
-                v = v + dot(OA[p, s], DYC[s, :, cols], 0, 0)
-            OWO[0, :, cols] = v[:E]
-            OWO[1, :, cols] = v[E:]
+        def body(t, _):
+            cols = pl.ds(mul(t, OT), OT)
+            v = dot(OA[p].reshape(NY * R, 2 * E), DYC[:, :, cols].reshape(NY * R, OT), 0, 0)
+            dwo_ref[2 * p, :, cols] = v[:E]
+            dwo_ref[2 * p + 1, :, cols] = v[E:]
             return 0
         lax.fori_loop(0, CW // OT, body, 0)
-        dwo_out(p).start()
 
     def dwq(p):
-        yopp(NP + p)
-        if p:
-            dwq_out(p - 1).wait()
-
-        def body(t, _):
-            cols = pl.ds(pl.multiple_of(t * NT, NT), NT)
-            v = dot(XC[0, :, cols], DQA[p, 0], 0, 0)
-            for s in range(1, NY):
-                v = v + dot(XC[s, :, cols], DQA[p, s], 0, 0)
-            OWQ[0, cols, :] = v[:, :E]
-            OWQ[1, cols, :] = v[:, E:]
-            return 0
-        lax.fori_loop(0, CW // NT, body, 0)
-        dwq_out(p).start()
+        def body(t, _):
+            cols = pl.ds(mul(t, OT), OT)
+            v = dot(XC[:, :, cols].reshape(NY * R, OT), DQA[p].reshape(NY * R, 2 * E), 0, 0)
+            dwq_ref[2 * p, cols, :] = v[:, :E]
+            dwq_ref[2 * p + 1, cols, :] = v[:, E:]
+            return 0
+        lax.fori_loop(0, CW // OT, body, 0)
 
     def own_cols(dst, src):
         def body(t, _):
@@ -455,59 +474,70 @@
                 copy_acc(DOB)
                 own_cols(DYC, DYS)
                 KVACC[...] = jnp.zeros_like(KVACC)
-                attn_bwd(0)
-                yown(NP)
-                yfwd(1)
-        elif i == 8:
-            attn_bwd(1)
-            yown(NP + 1)
-            attn_bwd(2)
-            yown(NP + 2)
-            for k in range(NY):
-                ag_sent(NY + k)
-            wait_send(DYS.at[0, pl.ds(0, 3 * T)], a2as.at[1])
-            dkv_send()
-            yfwd(2)
-        elif i == 9:
-            dkv_sum()
-            dxc(0)
-            dwkv_early()
-            dxc(1)
-        elif i == 10:
-            dxc(2)
-            rs1(0)
-            dxc(3)
-            rs1(1)
-            yfwd(NP)
-
-    for i in range(N_IT + 1):
-        if i < N_IT:
-            fwd(i)
-        if i + 2 < N_IT:
-            own(i + 2)
+
+    for i in range(9):
+        fwd(i)
+        for n in range(i + 2, N_IT if i == 7 else i + 3):
+            if n < N_IT and i <= 7:
+                own(n)
         if i >= 1:
             opp(i - 1)
-            if i - 1 < 2 * NY:
-                fin(i - 1)
+            fin(i - 1)
             compute(i - 1)
 
+    attn_bwd(0)
+    yown(NP)
+    fwd(9)
+    yfwd(1)
+    attn_bwd(1)
+    yown(NP + 1)
+    fwd(10)
+    attn_bwd(2)
+    yown(NP + 2)
+    for k in range(NY):
+        ag_sent(NY + k)
+    wait_send(DYS.at[0, pl.ds(0, 3 * T)], a2as.at[1])
+    dkv_send()
+    yfwd(2)
+    opp(8)
+    dkv_sum()
+    dwkv_early()
+    dxc(0)
+    fwd(11)
+    dwkv_part(0)
+    dwkv_part(1)
+    dwkv_own()
+    x_free()
+    yfwd(NP)
+    opp(9)
+    dxc(1)
+    pl.semaphore_wait(cred, 2)
+    rs1(0)
+    opp(10)
+    yfwd(NP + 1)
+    dxc(2)
+    rs1(1)
+    opp(11)
+    dxc(3)
     rs1(2)
     rs1(3)
-    yfwd(NP + 1)
+    yfwd(NP + 2)
+    rs2(0)
     dwkv_mid()
-    yfwd(NP + 2)
-    for i in range(2 * NY, 2 * NY + 3):
+    for i in range(2 * NY, N_IT):
         fin(i)
-    rs2(0)
+    for p in range(NP):
+        yopp(p)
     dwo(0)
     rs2(1)
     dwo(1)
     rs2(2)
     dwo(2)
     rs2(3)
-    xc_fin(0)
-    xc_fin(1)
-    fin(N_IT - 1)
+    for n in range(2):
+        xc_fin(n)
+    for p in range(NP):
+        yopp(NP + p)
     dwq(0)
     rs3(0)
     dwq(1)
@@ -517,11 +547,10 @@
     dwkv_final()
     rs3(3)
 
-    for i in list(range(NY)) + list(range(2 * NY, N_IT)):
+    for i in range(2 * NY, N_IT):
         ag_sent(i)
-    wait_send(XS.at[0, pl.ds(0, T)], a2as.at[0])
-    for n in range(4):
-        wait_send(XC.at[0, par], xcs.at[n])
+    for n in range(2):
+        wait_send(XC.at[0, par], xcs.at[2 + n])
     for q in range(2 * NP):
         ysent(q)
     wait_send(KVACC, exs.at[0])
@@ -529,11 +558,7 @@
         wait_send(KS.at[n], dks.at[n])
     for k in range(NY):
         wait_send(DYS.at[k, pl.ds(HR, HR)], pxs.at[k])
-        wait_send(SX.at[k], rss.at[k])
-        dx_out(k).wait()
-    dwkv_out_wait()
-    dwo_out(NP - 1).wait()
-    dwq_out(NP - 1).wait()
+        wait_send(XS.at[k, pl.ds(0, 3 * T)], rss.at[k])
 
 
 def solution(mesh):
@@ -559,23 +584,19 @@
             V((NY, R, CW), BF16), V((NY, R, CW), BF16), V((NY, R, CW), BF16), V((NY, R, CW), BF16),
             V((NP, NY, R, 2 * E), BF16), V((NP, NY, R, 2 * E), BF16),
             V((NP, R, 2 * E), BF16), V((NP, R, 2 * E), BF16), V((2, R, E), BF16),
-            V((NP, R, 2 * E), F32), V((R, 2 * E), F32), V((R, 2 * E), F32), V((2, R, E), BF16),
+            V((R, 2 * E), F32), V((R, 2 * E), F32), V((2, R, E), BF16),
             V((NH, CW, E), BF16), V((2, CW, E), BF16), V((NH, E, CW), BF16),
-            V((NY, R // 2, CW), F32), V((NY, 3 * T, CW), BF16), V((NY, 3 * T, CW), BF16), V((NY, T, CW), BF16),
-            V((NY - 1, KB, 2 * E), BF16), V((NY - 1, KB, 2 * E), BF16), V((2, KB, E), F32),
-            V((2, CW, E), F32), V((2, E, CW), F32),
+            V((NY, R // 2, CW), F32), V((NY - 1, KB, 2 * E), BF16), V((NY - 1, KB, 2 * E), BF16),
             S((n_it, 5)), S((n_it,)), S((NY,)), S((2,)), S((4,)), S((4,)), S((2 * NP, 4)), S((2 * NP,)),
             S((4,)), S((3,)), S((NY,)), S((NY,)), S((NY, 4)), S((NY,)), S((1,)), S((1,)),
-            S((NY,)), S((NY,)), S((1,)), S((2,)), S((1,)), S((4 + NY,)),
+            S((NY,)), S((NY,)), S((1,)), S((2,)), S((1,)), pltpu.SemaphoreType.REGULAR,
         ]
         any_spec = pl.BlockSpec(memory_space=pl.ANY)
         dx, dwq, dwk, dwv, dwo = pl.pallas_call(
             functools.partial(kernel, cfg),
-            out_shape=[jax.ShapeDtypeStruct((T, D), BF16), jax.ShapeDtypeStruct((NH, CW, E), F32),
-                       jax.ShapeDtypeStruct((KB, E), F32), jax.ShapeDtypeStruct((KB, E), F32),
-                       jax.ShapeDtypeStruct((NH, E, CW), F32)],
+            out_shape=[V((T, D), BF16), V((NH, CW, E), F32), V((KB, E), F32), V((KB, E), F32), V((NH, E, CW), F32)],
             in_specs=[any_spec] * 6,
-            out_specs=[any_spec] * 5,
+            out_specs=[pl.BlockSpec(memory_space=V)] * 5,
             scratch_shapes=scratch,
             compiler_params=pltpu.CompilerParams(collective_id=0, has_side_effects=True, vmem_limit_bytes=VMEM_BYTES),
             name='attn_bwd_fused',

time: 137 us -> 130 us (0.949)
  local copies, waits for them, and re-layouts: 10.8 us -> 6.74 us
  Pallas kernels: 125 us -> 123 us
    unnamed x13 -> x5, local copies, waits for them, and re-layouts: 10.8 us -> 6.74 us
    pallas_call x1, Pallas kernels: 125 us -> 123 us  [device_step(): pl.pallas_call(functools.partial(kernel, cfg), out_shape=[V((T, D), BF16)...]
where the time goes in v3:
time: 130 us
  Pallas kernels  123 us (95%)
  local copies, waits for them, and re-layouts  6.74 us (5%)
    pallas_call x1, Pallas kernels, device_step(): pl.pallas_call(functools.partial(kernel, cfg), out_shape=[V((T, D), BF16)...  123 us
    unnamed x5, local copies, waits for them, and re-layouts  6.74 us

profile of v3, /device:TPU:97, one launch (start us, length us, event | category | flops | bytes accessed | tf_op | source)
XLA Modules:
  0.0 130.3 jit_solution(5086368365604533181)
XLA Ops:
  0.6 122.9 %attn_bwd_fused.1 = (bf16[64,6144]{1,0:T(8,128)(2,1)S(1)}, f32[6,1536,128]{2,1,0:T(8,128)S(1)}, f32[768,128]{1,0:T(8,128)S(1)}, f32[768,128]{1,0:T(8,128)S(1)}, f32[6,128,1536]{2,1,0:T(8,128)S(1)}) custom-call(bf16[64,6144]{1,0:T(8,128)(2,1)} %bitcast.8, bf16[64,6144]{1,0:T(8,128)(2,1)} %bitcast.9, bf16[6,6144,128]{2,1,0:T(8,128)(2,1)} %bitcast.7, ...), custom_call_target="tpu_custom_call" | custom-call | tf_op jit(solution)/shard_map/attn_bwd_fused/pallas_call | solution.py:595
  123.5 0.9 copy.16
  124.4 2.2 %copy.17 = f32[1536,6,128]{2,0,1:T(8,128)} copy(f32[1536,6,128]{2,0,1:T(8,128)S(1)} %bitcast.5) | data formatting | bytes 9437184
  126.6 0.7 copy.18
  127.4 0.7 copy.19
  128.1 2.2 %copy.20 = f32[6,128,1536]{2,1,0:T(8,128)} copy(f32[6,128,1536]{2,1,0:T(8,128)S(1)} %get-tuple-element.19) | data formatting | bytes 9437184

commit v4 on v3

--- a/solution.py
+++ b/solution.py
@@ -11,6 +11,9 @@
 F32 = jnp.float32
 BF16 = jnp.bfloat16
 VMEM_BYTES = 54 * 1000 * 1000
+DXT = 384
+OUT_IN = pl.ANY
+OUT_LIM = 1024 * 1024
 LOG2E = 1.4426950408889634
 
 
@@ -25,7 +28,7 @@
 def kernel(cfg, x_ref, dy_ref, wq_ref, wk_ref, wv_ref, wo_ref,
            dx_ref, dwq_ref, dwk_ref, dwv_ref, dwo_ref,
            XS, DYS, XC, DYC, OA, DQA, QB, DOB, KV, KVACC, DKVR, DKVB,
-           WQ, WKV, WO, MY, KS, KR,
+           WQ, WKV, WO, MY, SX, KS, KR,
            agr, ags, a2ar, a2as, xcr, xcs, yr, ys, dkr, dks, pxr, pxs, rsr, rss, exs, exr,
            lx, ldy, lwq, lwkv, lwo, cred):
     T, CW, E, NX, NY, NH = cfg
@@ -350,68 +353,75 @@
             return 0
         lax.fori_loop(0, KB // KT, body, 0)
 
-    def x_free():
-        for i in range(NY):
-            ag_sent(i)
-        wait_send(XS.at[0, pl.ds(0, T)], a2as.at[0])
-        for n in range(2):
-            wait_send(XS.at[0, par], xcs.at[n])
+    def rx_free():
         for dev in (XL, XR):
             pl.semaphore_signal(cred, inc=1, device_id=dev, device_id_type=MESH)
 
-    NT = tile_of(CW, 256)
+    CH = CW // 2
+    NT = tile_of(CH, DXT)
+
+    def w_half(k, g):
+        rows, dst = pl.ds(k * CW + g * CH, CH), pl.ds(g * CH, CH)
+        return [pltpu.make_async_copy(wq_ref.at[:, rows, :], WQ.at[:, dst, :], lwq.at[1 + g]),
+                pltpu.make_async_copy(wk_ref.at[c, rows], WKV.at[0, dst], lwkv.at[2 + g]),
+                pltpu.make_async_copy(wv_ref.at[c, rows], WKV.at[1, dst], lwkv.at[4 + g])]
 
     def dxc(k):
-        wq_cp(k).wait()
-        for cp in wkv_cp(k):
-            cp.wait()
-
-        def body(t, _):
-            off = pl.multiple_of(t * NT, NT)
-            rows = pl.ds(off, NT)
-            w = jnp.concatenate([WQ[i, rows, :] for i in range(NH)] + [WKV[h, rows, :]], axis=1)
-            v = dot(jnp.concatenate([DQA[p, y] for p in range(NP)] + [DKVB[h]], axis=1), w, 1, 1)
-            lo, hi = v[:HR], v[HR:]
-            MY[k, :, pl.ds(off, NT)] = jnp.where(h == 0, lo, hi)
-            DYS[k, pl.ds(HR, HR), pl.ds(off, NT)] = jnp.where(h == 0, hi, lo).astype(BF16)
-            return 0
-        lax.fori_loop(0, CW // NT, body, 0)
-        if k + 1 < NY:
-            wq_cp(k + 1).start()
-            for cp in wkv_cp(k + 1):
-                cp.start()
+        if k == 0:
+            wq_cp(0).wait()
+            for cp in wkv_cp(0):
+                cp.wait()
+        for g in range(2):
+            if k:
+                for cp in w_half(k, g):
+                    cp.wait()
+
+            def body(t, _):
+                off = pl.multiple_of(t * NT + g * CH, NT)
+                rows = pl.ds(off, NT)
+                w = jnp.concatenate([WQ[i, rows, :] for i in range(NH)] + [WKV[h, rows, :]], axis=1)
+                v = dot(jnp.concatenate([DQA[p, y] for p in range(NP)] + [DKVB[h]], axis=1), w, 1, 1)
+                lo, hi = v[:HR], v[HR:]
+                MY[k, :, pl.ds(off, NT)] = jnp.where(h == 0, lo, hi)
+                DYS[k, pl.ds(HR, HR), pl.ds(off, NT)] = jnp.where(h == 0, hi, lo).astype(BF16)
+                return 0
+            lax.fori_loop(0, CH // NT, body, 0)
+            if k + 1 < NY:
+                for cp in w_half(k + 1, g):
+                    cp.start()
         rc(DYS.at[k, pl.ds(HR, HR)], DYS.at[k, pl.ds(0, HR)], pxs.at[k], pxr.at[k], PT).start()
-
-    RO = 3 * T
 
     def blk(k, cc, o, n):
         rows = pl.ds(pl.multiple_of(cc * T + o, TH), n)
         return MY[k, rows, :] + DYS[k, rows, :].astype(F32)
 
+    def rx_early(k, n):
+        return WO.at[n, k * TH:(k + 1) * TH]
+
+    def rx_full(k, n):
+        i = 2 * (k % 2)
+        return WO.at[2 + 2 * n + k // 2, i * TH:(i + 2) * TH]
+
     def rs1(k):
         wait_recv(DYS.at[k, pl.ds(0, HR)], pxr.at[k])
-        XS[k, 0:T, :] = blk(k, chip(2), 0, T).astype(BF16)
-        s, d = XS.at[k, pl.ds(0, TH)], XS.at[k, pl.ds(RO + 0, TH)]
-        rc(s, d, rss.at[k], rsr.at[k, 0], XR).start()
-        s, d = XS.at[k, pl.ds(TH, TH)], XS.at[k, pl.ds(RO + TH, TH)]
-        rc(s, d, rss.at[k], rsr.at[k, 1], XL).start()
+        SX[k, 0:T, :] = blk(k, chip(2), 0, T).astype(BF16)
+        for n, dev in enumerate((XR, XL)):
+            rc(SX.at[k, n * TH:(n + 1) * TH], rx_early(k, n), rss.at[k], rsr.at[k, n], dev).start()
 
     def rs2(k):
-        wait_recv(XS.at[k, pl.ds(RO + 0, TH)], rsr.at[k, 0])
-        XS[k, T:T + TH, :] = (blk(k, chip(1), 0, TH) + XS[k, RO + 0:RO + TH, :].astype(F32)).astype(BF16)
-        XS[k, T + TH:2 * T, :] = blk(k, chip(1), TH, TH).astype(BF16)
-        s, d = XS.at[k, pl.ds(T, T)], XS.at[k, pl.ds(RO + T, T)]
-        rc(s, d, rss.at[k], rsr.at[k, 2], XR).start()
-        wait_recv(XS.at[k, pl.ds(RO + TH, TH)], rsr.at[k, 1])
-        XS[k, 2 * T:2 * T + TH, :] = blk(k, chip(-1), 0, TH).astype(BF16)
-        XS[k, 2 * T + TH:3 * T, :] = (blk(k, chip(-1), TH, TH) + XS[k, RO + TH:RO + T, :].astype(F32)).astype(BF16)
-        s, d = XS.at[k, pl.ds(2 * T, T)], XS.at[k, pl.ds(RO + 2 * T, T)]
-        rc(s, d, rss.at[k], rsr.at[k, 3], XL).start()
+        for n, dev in enumerate((XR, XL)):
+            o = (n + 1) * T
+            add = slice(o + n * TH, o + (n + 1) * TH)
+            SX[k, o + (1 - n) * TH:o + (2 - n) * TH, :] = blk(k, chip(1 - 2 * n), (1 - n) * TH, TH).astype(BF16)
+            wait_recv(rx_early(k, n), rsr.at[k, n])
+            SX[k, add, :] = (blk(k, chip(1 - 2 * n), n * TH, TH) + rx_early(k, n)[...].astype(F32)).astype(BF16)
+            rc(SX.at[k, o:o + T], rx_full(k, n), rss.at[k], rsr.at[k, 2 + n], dev).start()
 
     def rs3(k):
-        wait_recv(XS.at[k, pl.ds(RO + T, T)], rsr.at[k, 2])
-        wait_recv(XS.at[k, pl.ds(RO + 2 * T, T)], rsr.at[k, 3])
-        v = blk(k, c, 0, T) + XS[k, RO + T:RO + 2 * T, :].astype(F32) + XS[k, RO + 2 * T:RO + 3 * T, :].astype(F32)
+        v = blk(k, c, 0, T)
+        for n in range(2):
+            wait_recv(rx_full(k, n), rsr.at[k, 2 + n])
+            v = v + rx_full(k, n)[...].astype(F32)
         dx_ref[:, k * CW:(k + 1) * CW] = v.astype(BF16)
 
     OT = tile_of(CW, 512)
@@ -444,11 +454,13 @@
     own(0)
     own(1)
     rc(XS.at[seq(2), pl.ds(my_rows, T)], XC.at[y, pl.ds(my_rows, T)], a2as.at[0], a2ar.at[3], at(2, 0)).start()
-    for cp in ldc:
-        cp.wait()
-    for j in range(1, NY):
-        rc(DYS.at[seq(j), pl.ds(my_rows, T)], DYC.at[y, pl.ds(my_rows, T)],
-           a2as.at[1], a2ar.at[NY - j - 1], at(j, 0)).start()
+
+    def dy_a2a():
+        for cp in ldc:
+            cp.wait()
+        for j in range(1, NY):
+            rc(DYS.at[seq(j), pl.ds(my_rows, T)], DYC.at[y, pl.ds(my_rows, T)],
+               a2as.at[1], a2ar.at[NY - j - 1], at(j, 0)).start()
 
     def compute(i):
         if i < NY:
@@ -471,12 +483,15 @@
                 xc_fwd(1)
                 yfwd(0)
             if i == 7:
+                rx_free()
                 copy_acc(DOB)
                 own_cols(DYC, DYS)
                 KVACC[...] = jnp.zeros_like(KVACC)
 
     for i in range(9):
         fwd(i)
+        if i == 0:
+            dy_a2a()
         for n in range(i + 2, N_IT if i == 7 else i + 3):
             if n < N_IT and i <= 7:
                 own(n)
@@ -499,58 +514,58 @@
     wait_send(DYS.at[0, pl.ds(0, 3 * T)], a2as.at[1])
     dkv_send()
     yfwd(2)
-    opp(8)
     dkv_sum()
-    dwkv_early()
     dxc(0)
     fwd(11)
-    dwkv_part(0)
-    dwkv_part(1)
-    dwkv_own()
-    x_free()
-    yfwd(NP)
-    opp(9)
     dxc(1)
     pl.semaphore_wait(cred, 2)
     rs1(0)
-    opp(10)
-    yfwd(NP + 1)
+    dwkv_early()
+    yfwd(NP)
     dxc(2)
     rs1(1)
-    opp(11)
+    rs2(0)
+    yfwd(NP + 1)
     dxc(3)
     rs1(2)
+    rs2(1)
     rs1(3)
+    dwkv_part(0)
+    dwkv_part(1)
+    for i in range(2 * NY, N_IT - 1):
+        opp(i)
     yfwd(NP + 2)
-    rs2(0)
-    dwkv_mid()
-    for i in range(2 * NY, N_IT):
+    for i in range(2 * NY, N_IT - 1):
         fin(i)
     for p in range(NP):
         yopp(p)
     dwo(0)
-    rs2(1)
+    rs2(2)
+    opp(N_IT - 1)
+    dwkv_mid()
     dwo(1)
-    rs2(2)
+    rs2(3)
     dwo(2)
-    rs2(3)
+    rs3(0)
     for n in range(2):
         xc_fin(n)
+    fin(N_IT - 1)
     for p in range(NP):
         yopp(NP + p)
     dwq(0)
-    rs3(0)
+    rs3(1)
+    dwkv_own()
     dwq(1)
-    rs3(1)
+    rs3(2)
     dwq(2)
-    rs3(2)
     dwkv_final()
     rs3(3)
 
-    for i in range(2 * NY, N_IT):
+    for i in list(range(NY)) + list(range(2 * NY, N_IT)):
         ag_sent(i)
-    for n in range(2):
-        wait_send(XC.at[0, par], xcs.at[2 + n])
+    wait_send(XS.at[0, pl.ds(0, T)], a2as.at[0])
+    for n in range(4):
+        wait_send(XC.at[0, par], xcs.at[n])
     for q in range(2 * NP):
         ysent(q)
     wait_send(KVACC, exs.at[0])
@@ -558,7 +573,16 @@
         wait_send(KS.at[n], dks.at[n])
     for k in range(NY):
         wait_send(DYS.at[k, pl.ds(HR, HR)], pxs.at[k])
-        wait_send(XS.at[k, pl.ds(0, 3 * T)], rss.at[k])
+        wait_send(SX.at[k], rss.at[k])
+
+
+def copy_out(*refs):
+    n = (len(refs) - 1) // 2
+    cps = [pltpu.make_async_copy(refs[i], refs[n + i], refs[-1].at[i]) for i in range(n)]
+    for cp in cps:
+        cp.start()
+    for cp in cps:
+        cp.wait()
 
 
 def solution(mesh):
@@ -571,7 +595,7 @@
         KVH = w_k.shape[0]
         NX = model_size // 2
         NY = mesh.shape['data']
-        assert NX == 4 and NY == 4 and KVH == NX and NH == 6
+        assert NX == 4 and NY == 4 and KVH == NX and NH == 6 and E == 2 * T
         NP = NH // 2
         CW = D // NY
         R = model_size * T
@@ -586,10 +610,10 @@
             V((NP, R, 2 * E), BF16), V((NP, R, 2 * E), BF16), V((2, R, E), BF16),
             V((R, 2 * E), F32), V((R, 2 * E), F32), V((2, R, E), BF16),
             V((NH, CW, E), BF16), V((2, CW, E), BF16), V((NH, E, CW), BF16),
-            V((NY, R // 2, CW), F32), V((NY - 1, KB, 2 * E), BF16), V((NY - 1, KB, 2 * E), BF16),
+            V((NY, R // 2, CW), F32), V((NY, 3 * T, CW), BF16), V((NY - 1, KB, 2 * E), BF16), V((NY - 1, KB, 2 * E), BF16),
             S((n_it, 5)), S((n_it,)), S((NY,)), S((2,)), S((4,)), S((4,)), S((2 * NP, 4)), S((2 * NP,)),
             S((4,)), S((3,)), S((NY,)), S((NY,)), S((NY, 4)), S((NY,)), S((1,)), S((1,)),
-            S((NY,)), S((NY,)), S((1,)), S((2,)), S((1,)), pltpu.SemaphoreType.REGULAR,
+            S((NY,)), S((NY,)), S((3,)), S((6,)), S((1,)), pltpu.SemaphoreType.REGULAR,
         ]
         any_spec = pl.BlockSpec(memory_space=pl.ANY)
         dx, dwq, dwk, dwv, dwo = pl.pallas_call(
@@ -601,6 +625,16 @@
             compiler_params=pltpu.CompilerParams(collective_id=0, has_side_effects=True, vmem_limit_bytes=VMEM_BYTES),
             name='attn_bwd_fused',
         )(x_loc[0], dy_loc[0], w_q.transpose(1, 0, 2), w_k, w_v, w_o)
+        outs = (dx, dwq, dwk, dwv, dwo)
+        dx, dwq, dwk, dwv, dwo = pl.pallas_call(
+            copy_out,
+            out_shape=[jax.ShapeDtypeStruct(o.shape, o.dtype) for o in outs],
+            in_specs=[pl.BlockSpec(memory_space=OUT_IN)] * 5,
+            out_specs=[any_spec] * 5,
+            scratch_shapes=[S((5,))],
+            compiler_params=pltpu.CompilerParams(vmem_limit_bytes=OUT_LIM),
+            name='write_results',
+        )(*outs)
         return dx[None], dwq.transpose(1, 0, 2), dwk, dwv, dwo
 
     kv_rows = P(('pod', 'model', 'data'), None)

time: 130 us -> 124 us (0.954); the launches traced: 130 us -> 123 us
  local copies, waits for them, and re-layouts: 6.74 us -> 0 us
    unnamed x5 -> x0, local copies, waits for them, and re-layouts: 6.74 us -> none
    pallas_call x1, Pallas kernels: 123 us -> 118 us  [device_step(): pl.pallas_call(functools.partial(kernel, cfg), out_shape=[V((T, D), BF16)...]
    pallas_call x0 -> x1, Pallas kernels: none -> 4.28 us  [device_step(): pl.pallas_call(copy_out, out_shape=[jax.ShapeDtypeStruct(o.shape, o.dtype...]
where the time goes in v4:
time: 124 us; the launch traced here: 123 us
  Pallas kernels  122 us (98%)
    pallas_call x1, Pallas kernels, device_step(): pl.pallas_call(functools.partial(kernel, cfg), out_shape=[V((T, D), BF16)...  118 us
    pallas_call x1, Pallas kernels, device_step(): pl.pallas_call(copy_out, out_shape=[jax.ShapeDtypeStruct(o.shape, o.dtype...  4.28 us

profile of v4, /device:TPU:97, one launch (start us, length us, event | category | flops | bytes accessed | tf_op | source)
XLA Modules:
  0.0 122.7 jit_solution(12468187777451458639)
XLA Ops:
  0.6 117.5 %attn_bwd_fused.1 = (bf16[64,6144]{1,0:T(8,128)(2,1)S(1)}, f32[6,1536,128]{2,1,0:T(8,128)S(1)}, f32[768,128]{1,0:T(8,128)S(1)}, f32[768,128]{1,0:T(8,128)S(1)}, f32[6,128,1536]{2,1,0:T(8,128)S(1)}) custom-call(bf16[64,6144]{1,0:T(8,128)(2,1)} %bitcast.6, bf16[64,6144]{1,0:T(8,128)(2,1)} %bitcast.7, bf16[6,6144,128]{2,1,0:T(8,128)(2,1)} %bitcast.5, ...), custom_call_target="tpu_custom_call" | custom-call | tf_op jit(solution)/shard_map/attn_bwd_fused/pallas_call | solution.py:619
  118.2 4.3 %write_results.1 = (bf16[64,6144]{1,0:T(8,128)(2,1)}, f32[6,1536,128]{2,1,0:T(8,128)}, f32[768,128]{1,0:T(8,128)}, f32[768,128]{1,0:T(8,128)}, f32[6,128,1536]{2,1,0:T(8,128)}) custom-call(bf16[64,6144]{1,0:T(8,128)(2,1)S(1)} %get-tuple-element.15.refs_0_, f32[6,1536,128]{2,1,0:T(8,128)S(1)} %get-tuple-element.16.refs_1_, ...), custom_call_target="tpu_custom_call" | custom-call | tf_op jit(solution)/shard_map/write_results/pallas_call | solution.py:629

commit v5 on v4

--- a/solution.py
+++ b/solution.py
@@ -10,8 +10,10 @@
 MESH = pl.DeviceIdType.MESH
 F32 = jnp.float32
 BF16 = jnp.bfloat16
-VMEM_BYTES = 54 * 1000 * 1000
+VMEM_BYTES = 55 * 1000 * 1000
 DXT = 384
+KTW = 768
+UNR = True
 OUT_IN = pl.ANY
 OUT_LIM = 1024 * 1024
 LOG2E = 1.4426950408889634
@@ -28,8 +30,8 @@
 def kernel(cfg, x_ref, dy_ref, wq_ref, wk_ref, wv_ref, wo_ref,
            dx_ref, dwq_ref, dwk_ref, dwv_ref, dwo_ref,
            XS, DYS, XC, DYC, OA, DQA, QB, DOB, KV, KVACC, DKVR, DKVB,
-           WQ, WKV, WO, MY, SX, KS, KR,
-           agr, ags, a2ar, a2as, xcr, xcs, yr, ys, dkr, dks, pxr, pxs, rsr, rss, exs, exr,
+           WQ, WKV, WO, MY, SX, KS, KR, ST,
+           agr, ags, a2ar, a2as, str_, sts, xcr, xcs, yr, ys, dkr, dks, pxr, pxs, rsr, rss, exs, exr,
            lx, ldy, lwq, lwkv, lwo, cred):
     T, CW, E, NX, NY, NH = cfg
     NP = NH // 2
@@ -82,35 +84,50 @@
                 pltpu.make_async_copy(wv_ref.at[c, pl.ds(mul(k, CW), CW)], WKV.at[1], lwkv.at[1])]
 
     def wo_cp(k):
-        return pltpu.make_async_copy(wo_ref.at[:, :, pl.ds(k * CW, CW)], WO, lwo.at[0])
+        return pltpu.make_async_copy(wo_ref.at[:, :, pl.ds(mul(k, CW), CW)], WO, lwo.at[0])
 
     bar = pltpu.get_barrier_semaphore()
     peers = [XR, XL, PT] + [at(j, 0) for j in range(1, NY)]
     for dev in peers:
         pl.semaphore_signal(bar, inc=1, device_id=dev, device_id_type=MESH)
     x_order = [seq(1), seq(-1), seq(2), y]
+    dy_order = [y, seq(1), seq(-1), seq(2)]
     lxc = [pltpu.make_async_copy(x_ref.at[:, pl.ds(k * CW, CW)], XS.at[k, pl.ds(my_rows, T)], lx.at[k]) for k in range(NY)]
     ldc = [pltpu.make_async_copy(dy_ref.at[:, pl.ds(k * CW, CW)], DYS.at[k, pl.ds(my_rows, T)], ldy.at[k]) for k in range(NY)]
-    for cp in lxc:
+    for cp in lxc + ldc:
         cp.start()
     for cp in lxc:
         cp.wait()
-    for cp in ldc:
-        cp.start()
     wq_cp(x_order[0]).start()
     for cp in wkv_cp(x_order[0]):
         cp.start()
-    wo_cp(0).start()
+    wo_cp(dy_order[0]).start()
     pl.semaphore_wait(bar, len(peers))
 
-    items = ([(XS, k) for k in x_order] + [(DYS, k) for k in range(NY)]
+    items = ([(XS, k) for k in x_order] + [(DYS, k) for k in dy_order]
              + [(DYC, seq(j)) for j in range(1, NY)] + [(XC, seq(2))])
     N_IT = len(items)
+
+    def my_half(n):
+        return pl.ds(pl.multiple_of(my_rows + n * TH, TH), TH)
+
+    def far_send(t):
+        for n, dev in enumerate((YU, YD)):
+            rc((DYS, XS)[t].at[seq(2), my_half(n)], ST.at[t, n], sts.at[t, n], str_.at[t, n], dev).start()
+
+    def far_fwd(t):
+        for n, dev in enumerate((YU, YD)):
+            wait_recv(ST.at[t, n], str_.at[t, n])
+            rc(ST.at[t, n], (DYC, XC)[t].at[seq((-1, 1)[n]), my_half(n)], sts.at[t, 2 + n], str_.at[t, 2 + n], dev).start()
 
     def own(i):
         buf, ix = items[i]
         if i >= 2 * NY:
-            wait_recv(buf.at[ix, pl.ds(my_rows, T)], a2ar.at[i - 2 * NY])
+            if i in (2 * NY + 1, 2 * NY + 3):
+                for n in range(2):
+                    wait_recv(buf.at[ix, my_half(n)], str_.at[(i - 2 * NY - 1) // 2, 2 + n])
+            else:
+                wait_recv(buf.at[ix, pl.ds(my_rows, T)], a2ar.at[i - 2 * NY])
         blk = buf.at[ix, pl.ds(my_rows, T)]
         rc(blk, blk, ags.at[i], agr.at[i, 0], XR).start()
         rc(blk, blk, ags.at[i], agr.at[i, 1], XL).start()
@@ -207,16 +224,17 @@
         for cp in wkv_cp(nk):
             cp.start()
 
-    def proj_dy(k):
+    def proj_dy(i):
+        k = dy_order[i]
         wo_cp(k).wait()
 
         def body(p, _):
             w = WO[pl.ds(2 * p, 2)].reshape(2 * E, CW)
-            acc(p, dot(DYS[k], w, 1, 1), k == 0)
-            return 0
-        lax.fori_loop(0, NP, body, 0)
-        if k + 1 < NY:
-            wo_cp(k + 1).start()
+            acc(p, dot(DYS[k], w, 1, 1), i == 0)
+            return 0
+        lax.fori_loop(0, NP, body, 0, unroll=UNR if i == NY - 1 else None)
+        if i + 1 < NY:
+            wo_cp(dy_order[i + 1]).start()
 
     def copy_acc(dst):
         def body(p, _):
@@ -255,11 +273,17 @@
         e = jnp.exp2(s - jnp.max(s, axis=1, keepdims=True))
         return e * (1.0 / jnp.sum(e, axis=1, keepdims=True))
 
+    def prow(g, b):
+        r = (g * T2 * 2 // E + b) * HR
+        return slice(r, r + HR)
+
     def attn_fwd(p):
         for g in range(2):
             for a in range(2):
                 ln = slice(a * E, (a + 1) * E)
                 pr = probs(pick(lambda r: QB[p, r, ln], g), g)
+                for b in range(pr.shape[1] // E):
+                    dwq_ref[2 * p + a, prow(g, b), :] = pr[:, b * E:(b + 1) * E]
                 o = dot(pr.astype(BF16), keys(1, g), 1, 0).astype(BF16)
 
                 def store(r, v):
@@ -273,7 +297,7 @@
                 q = pick(lambda r: QB[p, r, ln], g)
                 do = pick(lambda r: DOB[p, r, ln], g)
                 o = pick(lambda r: OA[p, y, r, ln], g)
-                pr = probs(q, g)
+                pr = jnp.concatenate([dwq_ref[2 * p + a, prow(g, b), :] for b in range((2 + 2 * g) * T2 // E)], axis=1)
                 delta = jnp.sum(do.astype(F32) * o.astype(F32), axis=1, keepdims=True)
                 dp = dot(do, keys(1, g), 1, 1)
                 ds = (pr * (dp - delta)).astype(BF16)
@@ -301,7 +325,7 @@
         DKVB[1] = tot[:, E:]
 
     KB = CW // 2
-    KT = tile_of(KB, 256)
+    KT = tile_of(KB, KTW)
 
     def dwkv_tile(r, t):
         ck = 2 * h + lax.div(r, 2)
@@ -385,7 +409,7 @@
                 MY[k, :, pl.ds(off, NT)] = jnp.where(h == 0, lo, hi)
                 DYS[k, pl.ds(HR, HR), pl.ds(off, NT)] = jnp.where(h == 0, hi, lo).astype(BF16)
                 return 0
-            lax.fori_loop(0, CH // NT, body, 0)
+            lax.fori_loop(0, CH // NT, body, 0, unroll=UNR)
             if k + 1 < NY:
                 for cp in w_half(k + 1, g):
                     cp.start()
@@ -426,24 +450,46 @@
 
     OT = tile_of(CW, 512)
 
-    def dwo(p):
+    others = [seq(1), seq(-1), seq(2)]
+
+    def dwo_own(p):
         def body(t, _):
             cols = pl.ds(mul(t, OT), OT)
-            v = dot(OA[p].reshape(NY * R, 2 * E), DYC[:, :, cols].reshape(NY * R, OT), 0, 0)
+            v = dot(OA[p, y], DYC[y, :, cols], 0, 0)
             dwo_ref[2 * p, :, cols] = v[:E]
             dwo_ref[2 * p + 1, :, cols] = v[E:]
             return 0
         lax.fori_loop(0, CW // OT, body, 0)
 
-    def dwq(p):
+    def dwo(p):
         def body(t, _):
             cols = pl.ds(mul(t, OT), OT)
-            v = dot(XC[:, :, cols].reshape(NY * R, OT), DQA[p].reshape(NY * R, 2 * E), 0, 0)
+            v = dot(jnp.concatenate([OA[p, s] for s in others], axis=0),
+                    jnp.concatenate([DYC[s, :, cols] for s in others], axis=0), 0, 0)
+            dwo_ref[2 * p, :, cols] = dwo_ref[2 * p, :, cols] + v[:E]
+            dwo_ref[2 * p + 1, :, cols] = dwo_ref[2 * p + 1, :, cols] + v[E:]
+            return 0
+        lax.fori_loop(0, CW // OT, body, 0)
+
+    def dwq_own(p):
+        def body(t, _):
+            cols = pl.ds(mul(t, OT), OT)
+            v = dot(XC[y, :, cols], DQA[p, y], 0, 0)
             dwq_ref[2 * p, cols, :] = v[:, :E]
             dwq_ref[2 * p + 1, cols, :] = v[:, E:]
             return 0
         lax.fori_loop(0, CW // OT, body, 0)
 
+    def dwq(p):
+        def body(t, _):
+            cols = pl.ds(mul(t, OT), OT)
+            v = dot(jnp.concatenate([XC[s, :, cols] for s in others], axis=0),
+                    jnp.concatenate([DQA[p, s] for s in others], axis=0), 0, 0)
+            dwq_ref[2 * p, cols, :] = dwq_ref[2 * p, cols, :] + v[:, :E]
+            dwq_ref[2 * p + 1, cols, :] = dwq_ref[2 * p + 1, cols, :] + v[:, E:]
+            return 0
+        lax.fori_loop(0, CW // OT, body, 0)
+
     def own_cols(dst, src):
         def body(t, _):
             rows = pl.ds(pl.multiple_of(t * T, T), T)
@@ -453,14 +499,13 @@
 
     own(0)
     own(1)
-    rc(XS.at[seq(2), pl.ds(my_rows, T)], XC.at[y, pl.ds(my_rows, T)], a2as.at[0], a2ar.at[3], at(2, 0)).start()
-
-    def dy_a2a():
-        for cp in ldc:
-            cp.wait()
-        for j in range(1, NY):
-            rc(DYS.at[seq(j), pl.ds(my_rows, T)], DYC.at[y, pl.ds(my_rows, T)],
-               a2as.at[1], a2ar.at[NY - j - 1], at(j, 0)).start()
+    far_send(1)
+    for cp in ldc:
+        cp.wait()
+    far_send(0)
+    for j, dev in ((1, YU), (-1, YD)):
+        rc(DYS.at[seq(j), pl.ds(my_rows, T)], DYC.at[y, pl.ds(my_rows, T)],
+           a2as.at[0], a2ar.at[1 + j], dev).start()
 
     def compute(i):
         if i < NY:
@@ -474,27 +519,38 @@
                 for p in range(NP):
                     attn_fwd(p)
                     yown(p)
+                    if p == 0:
+                        fwd(5)
+                        own(7)
                 own_cols(XC, XS)
         elif i < 8:
             proj_dy(i - NY)
+            if i == 4:
+                own_cols(DYC, DYS)
             if i == 5:
                 xc_fwd(0)
+                yfwd(0)
+                dwo_own(0)
+                dwo_own(1)
             if i == 6:
                 xc_fwd(1)
-                yfwd(0)
+                yfwd(1)
+                dwo_own(2)
             if i == 7:
                 rx_free()
+                yfwd(2)
                 copy_acc(DOB)
-                own_cols(DYC, DYS)
                 KVACC[...] = jnp.zeros_like(KVACC)
 
     for i in range(9):
-        fwd(i)
+        if i < 8 and i != 5:
+            fwd(i)
         if i == 0:
-            dy_a2a()
-        for n in range(i + 2, N_IT if i == 7 else i + 3):
-            if n < N_IT and i <= 7:
-                own(n)
+            far_fwd(1)
+        if i == 1:
+            far_fwd(0)
+        for n in range(i + 2, i + 3) if i < 5 else range(8, N_IT) if i == 7 else ():
+            own(n)
         if i >= 1:
             opp(i - 1)
             fin(i - 1)
@@ -502,68 +558,75 @@
 
     attn_bwd(0)
     yown(NP)
-    fwd(9)
-    yfwd(1)
+    fwd(8)
     attn_bwd(1)
     yown(NP + 1)
-    fwd(10)
     attn_bwd(2)
     yown(NP + 2)
+    fwd(9)
     for k in range(NY):
         ag_sent(NY + k)
-    wait_send(DYS.at[0, pl.ds(0, 3 * T)], a2as.at[1])
+    wait_send(DYS.at[0, pl.ds(0, 2 * T)], a2as.at[0])
+    for n in range(2):
+        wait_send(DYS.at[0, pl.ds(0, TH)], sts.at[0, n])
     dkv_send()
-    yfwd(2)
+    for p in range(NP):
+        dwq_own(p)
+    fwd(10)
     dkv_sum()
     dxc(0)
+    yfwd(NP)
+    dxc(1)
     fwd(11)
-    dxc(1)
     pl.semaphore_wait(cred, 2)
     rs1(0)
+    opp(8)
     dwkv_early()
-    yfwd(NP)
     dxc(2)
     rs1(1)
-    rs2(0)
     yfwd(NP + 1)
+    opp(9)
+    dwkv_part(0)
     dxc(3)
     rs1(2)
+    rs2(0)
+    opp(10)
+    yfwd(NP + 2)
+    dwkv_part(1)
+    rs1(3)
     rs2(1)
-    rs1(3)
-    dwkv_part(0)
-    dwkv_part(1)
-    for i in range(2 * NY, N_IT - 1):
-        opp(i)
-    yfwd(NP + 2)
+    opp(11)
     for i in range(2 * NY, N_IT - 1):
         fin(i)
     for p in range(NP):
         yopp(p)
-    dwo(0)
+        dwo(p)
+        if p == 1:
+            dwkv_mid()
     rs2(2)
-    opp(N_IT - 1)
-    dwkv_mid()
-    dwo(1)
-    rs2(3)
-    dwo(2)
-    rs3(0)
     for n in range(2):
         xc_fin(n)
     fin(N_IT - 1)
-    for p in range(NP):
-        yopp(NP + p)
+    yopp(NP)
     dwq(0)
+    dwkv_own()
+    rs3(0)
+    yopp(NP + 1)
+    dwq(1)
+    rs2(3)
     rs3(1)
-    dwkv_own()
-    dwq(1)
+    yopp(NP + 2)
+    dwq(2)
     rs3(2)
-    dwq(2)
     dwkv_final()
     rs3(3)
 
     for i in list(range(NY)) + list(range(2 * NY, N_IT)):
         ag_sent(i)
-    wait_send(XS.at[0, pl.ds(0, T)], a2as.at[0])
+    for n in range(2):
+        wait_send(XS.at[0, pl.ds(0, TH)], sts.at[1, n])
+        for t in range(2):
+            wait_send(ST.at[t, n], sts.at[t, 2 + n])
     for n in range(4):
         wait_send(XC.at[0, par], xcs.at[n])
     for q in range(2 * NP):
@@ -598,6 +661,7 @@
         assert NX == 4 and NY == 4 and KVH == NX and NH == 6 and E == 2 * T
         NP = NH // 2
         CW = D // NY
+        assert CW == 6 * NX * T
         R = model_size * T
         KB = CW // 2
         cfg = (T, CW, E, NX, NY, NH)
@@ -611,7 +675,8 @@
             V((R, 2 * E), F32), V((R, 2 * E), F32), V((2, R, E), BF16),
             V((NH, CW, E), BF16), V((2, CW, E), BF16), V((NH, E, CW), BF16),
             V((NY, R // 2, CW), F32), V((NY, 3 * T, CW), BF16), V((NY - 1, KB, 2 * E), BF16), V((NY - 1, KB, 2 * E), BF16),
-            S((n_it, 5)), S((n_it,)), S((NY,)), S((2,)), S((4,)), S((4,)), S((2 * NP, 4)), S((2 * NP,)),
+            V((2, 2, T // 2, CW), BF16),
+            S((n_it, 5)), S((n_it,)), S((NY,)), S((1,)), S((2, 4)), S((2, 4)), S((4,)), S((4,)), S((2 * NP, 4)), S((2 * NP,)),
             S((4,)), S((3,)), S((NY,)), S((NY,)), S((NY, 4)), S((NY,)), S((1,)), S((1,)),
             S((NY,)), S((NY,)), S((3,)), S((6,)), S((1,)), pltpu.SemaphoreType.REGULAR,
         ]

time: 124 us -> 120 us (0.968)
  Pallas kernels: 122 us -> 119 us
    pallas_call x1, Pallas kernels: 118 us -> 114 us  [device_step(): pl.pallas_call(functools.partial(kernel, cfg), out_shape=[V((T, D), BF16)...]
where the time goes in v5:
time: 120 us; the launch traced here: 119 us
  Pallas kernels  119 us (99%)
    pallas_call x1, Pallas kernels, device_step(): pl.pallas_call(functools.partial(kernel, cfg), out_shape=[V((T, D), BF16)...  114 us
    pallas_call x1, Pallas kernels, device_step(): pl.pallas_call(copy_out, out_shape=[jax.ShapeDtypeStruct(o.shape, o.dtype...  4.28 us

profile of v5, /device:TPU:97, one launch (start us, length us, event | category | flops | bytes accessed | tf_op | source)
XLA Modules:
  0.0 119.4 jit_solution(774067576857074767)
XLA Ops:
  0.6 114.3 %attn_bwd_fused.1 = (bf16[64,6144]{1,0:T(8,128)(2,1)S(1)}, f32[6,1536,128]{2,1,0:T(8,128)S(1)}, f32[768,128]{1,0:T(8,128)S(1)}, f32[768,128]{1,0:T(8,128)S(1)}, f32[6,128,1536]{2,1,0:T(8,128)S(1)}) custom-call(bf16[64,6144]{1,0:T(8,128)(2,1)} %bitcast.6, bf16[64,6144]{1,0:T(8,128)(2,1)} %bitcast.7, bf16[6,6144,128]{2,1,0:T(8,128)(2,1)} %bitcast.5, ...), custom_call_target="tpu_custom_call" | custom-call | tf_op jit(solution)/shard_map/attn_bwd_fused/pallas_call | solution.py:684
  114.9 4.3 %write_results.1 = (bf16[64,6144]{1,0:T(8,128)(2,1)}, f32[6,1536,128]{2,1,0:T(8,128)}, f32[768,128]{1,0:T(8,128)}, f32[768,128]{1,0:T(8,128)}, f32[6,128,1536]{2,1,0:T(8,128)}) custom-call(bf16[64,6144]{1,0:T(8,128)(2,1)S(1)} %get-tuple-element.15.refs_0_, f32[6,1536,128]{2,1,0:T(8,128)S(1)} %get-tuple-element.16.refs_1_, ...), custom_call_target="tpu_custom_call" | custom-call | tf_op jit(solution)/shard_map/write_results/pallas_call | solution.py:694

commit v6 on v5

--- a/solution.py
+++ b/solution.py
@@ -19,8 +19,20 @@
 LOG2E = 1.4426950408889634
 
 
-def dot(a, b, ca, cb):
+def dot(ca, cb, a, b):
     return lax.dot_general(a, b, (((ca,), (cb,)), ((), ())), preferred_element_type=F32)
+
+
+nn = functools.partial(dot, 1, 0)
+nt = functools.partial(dot, 1, 1)
+tn = functools.partial(dot, 0, 0)
+
+
+def loop(n, body, unroll=None):
+    def step(t, z):
+        body(t)
+        return z
+    lax.fori_loop(0, n, step, 0, unroll=unroll)
 
 
 def tile_of(n, t):
@@ -212,12 +224,11 @@
         for cp in wkv_cp(k):
             cp.wait()
 
-        def body(p, _):
+        def body(p):
             w = jnp.concatenate([WQ[2 * p], WQ[2 * p + 1]], axis=1)
-            acc(p, dot(XS[k], w, 1, 0), i == 0)
-            return 0
-        lax.fori_loop(0, NP, body, 0)
-        d = dot(XS[k], jnp.concatenate([WKV[0], WKV[1]], axis=1), 1, 0)
+            acc(p, nn(XS[k], w), i == 0)
+        loop(NP, body)
+        d = nn(XS[k], jnp.concatenate([WKV[0], WKV[1]], axis=1))
         KVACC[...] = d if i == 0 else KVACC[...] + d
         nk = x_order[i + 1] if i + 1 < NY else 0
         wq_cp(nk).start()
@@ -228,21 +239,19 @@
         k = dy_order[i]
         wo_cp(k).wait()
 
-        def body(p, _):
+        def body(p):
             w = WO[pl.ds(2 * p, 2)].reshape(2 * E, CW)
-            acc(p, dot(DYS[k], w, 1, 1), i == 0)
-            return 0
-        lax.fori_loop(0, NP, body, 0, unroll=UNR if i == NY - 1 else None)
+            acc(p, nt(DYS[k], w), i == 0)
+        loop(NP, body, unroll=UNR if i == NY - 1 else None)
         if i + 1 < NY:
             wo_cp(dy_order[i + 1]).start()
 
     def copy_acc(dst):
-        def body(p, _):
+        def body(p):
             cols = pl.ds(mul(p, 2 * E), 2 * E)
             dst[p, 0:HR, :] = MY[0, :, cols].astype(BF16)
             dst[p, HR:R, :] = MY[1, :, cols].astype(BF16)
-            return 0
-        lax.fori_loop(0, NP, body, 0)
+        loop(NP, body)
 
     T2 = 2 * T
 
@@ -264,7 +273,7 @@
         return pick(lambda r: KV[t, r, :], 0) if g == 0 else KV[t]
 
     def probs(q, g):
-        s = dot(q, keys(0, g), 1, 1) * scale2
+        s = nt(q, keys(0, g)) * scale2
         n = s.shape[1]
         qp = pos(brow(lax.broadcasted_iota(jnp.int32, (HR, 1), 0), g))
         kp = lax.broadcasted_iota(jnp.int32, (1, n), 1)
@@ -284,7 +293,7 @@
                 pr = probs(pick(lambda r: QB[p, r, ln], g), g)
                 for b in range(pr.shape[1] // E):
                     dwq_ref[2 * p + a, prow(g, b), :] = pr[:, b * E:(b + 1) * E]
-                o = dot(pr.astype(BF16), keys(1, g), 1, 0).astype(BF16)
+                o = nn(pr.astype(BF16), keys(1, g)).astype(BF16)
 
                 def store(r, v):
                     OA[p, y, r, ln] = v
@@ -299,10 +308,10 @@
                 o = pick(lambda r: OA[p, y, r, ln], g)
                 pr = jnp.concatenate([dwq_ref[2 * p + a, prow(g, b), :] for b in range((2 + 2 * g) * T2 // E)], axis=1)
                 delta = jnp.sum(do.astype(F32) * o.astype(F32), axis=1, keepdims=True)
-                dp = dot(do, keys(1, g), 1, 1)
+                dp = nt(do, keys(1, g))
                 ds = (pr * (dp - delta)).astype(BF16)
-                dq = (dot(ds, keys(0, g), 1, 0) * scale).astype(BF16)
-                dkv = jnp.concatenate([dot(ds, q, 0, 0), dot(pr.astype(BF16), do, 0, 0)], axis=1)
+                dq = (nn(ds, keys(0, g)) * scale).astype(BF16)
+                dkv = jnp.concatenate([tn(ds, q), tn(pr.astype(BF16), do)], axis=1)
 
                 def store(r, v):
                     DQA[p, y, r, ln] = v
@@ -331,32 +340,29 @@
         ck = 2 * h + lax.div(r, 2)
         off = pl.multiple_of(KB * lax.rem(r, 2) + t * KT, KT)
         kv = jnp.concatenate([DKVB[0], DKVB[1]], axis=1)
-        return dot(XS[ck, :, pl.ds(off, KT)], kv, 0, 0)
+        return tn(XS[ck, :, pl.ds(off, KT)], kv)
 
     KH = KB // 2
 
     def dwkv_early():
-        def body(t, _):
+        def body(t):
             KS[0, pl.ds(mul(t, KT), KT), :] = dwkv_tile(seq(2), t).astype(BF16)
-            return 0
-        lax.fori_loop(0, KB // KT, body, 0)
+        loop(KB // KT, body)
         rc(KS.at[0, pl.ds(0, KH)], KR.at[0, pl.ds(0, KH)], dks.at[0], dkr.at[0], YU).start()
         rc(KS.at[0, pl.ds(KH, KH)], KR.at[0, pl.ds(KH, KH)], dks.at[0], dkr.at[1], YD).start()
 
     def dwkv_part(n):
-        def body(t, _):
+        def body(t):
             KS[n + 1, pl.ds(mul(t, KT), KT), :] = dwkv_tile(seq((1, -1)[n]), t).astype(BF16)
-            return 0
-        lax.fori_loop(0, KB // KT, body, 0)
+        loop(KB // KT, body)
 
     def dwkv_own():
-        def body(t, _):
+        def body(t):
             rows = pl.ds(mul(t, KT), KT)
             v = dwkv_tile(y, t)
             dwk_ref[rows, :] = v[:, :E]
             dwv_ref[rows, :] = v[:, E:]
-            return 0
-        lax.fori_loop(0, KB // KT, body, 0)
+        loop(KB // KT, body)
 
     def dwkv_mid():
         for n, dev in enumerate((YU, YD)):
@@ -369,13 +375,12 @@
         for n in range(2):
             wait_recv(KR.at[n + 1], dkr.at[n + 2])
 
-        def body(t, _):
+        def body(t):
             rows = pl.ds(mul(t, KT), KT)
             v = KR[1, rows, :].astype(F32) + KR[2, rows, :].astype(F32)
             dwk_ref[rows, :] = dwk_ref[rows, :] + v[:, :E]
             dwv_ref[rows, :] = dwv_ref[rows, :] + v[:, E:]
-            return 0
-        lax.fori_loop(0, KB // KT, body, 0)
+        loop(KB // KT, body)
 
     def rx_free():
         for dev in (XL, XR):
@@ -400,16 +405,15 @@
                 for cp in w_half(k, g):
                     cp.wait()
 
-            def body(t, _):
+            def body(t):
                 off = pl.multiple_of(t * NT + g * CH, NT)
                 rows = pl.ds(off, NT)
                 w = jnp.concatenate([WQ[i, rows, :] for i in range(NH)] + [WKV[h, rows, :]], axis=1)
-                v = dot(jnp.concatenate([DQA[p, y] for p in range(NP)] + [DKVB[h]], axis=1), w, 1, 1)
+                v = nt(jnp.concatenate([DQA[p, y] for p in range(NP)] + [DKVB[h]], axis=1), w)
                 lo, hi = v[:HR], v[HR:]
                 MY[k, :, pl.ds(off, NT)] = jnp.where(h == 0, lo, hi)
                 DYS[k, pl.ds(HR, HR), pl.ds(off, NT)] = jnp.where(h == 0, hi, lo).astype(BF16)
-                return 0
-            lax.fori_loop(0, CH // NT, body, 0, unroll=UNR)
+            loop(CH // NT, body, unroll=UNR)
             if k + 1 < NY:
                 for cp in w_half(k + 1, g):
                     cp.start()
@@ -453,49 +457,44 @@
     others = [seq(1), seq(-1), seq(2)]
 
     def dwo_own(p):
-        def body(t, _):
+        def body(t):
             cols = pl.ds(mul(t, OT), OT)
-            v = dot(OA[p, y], DYC[y, :, cols], 0, 0)
+            v = tn(OA[p, y], DYC[y, :, cols])
             dwo_ref[2 * p, :, cols] = v[:E]
             dwo_ref[2 * p + 1, :, cols] = v[E:]
-            return 0
-        lax.fori_loop(0, CW // OT, body, 0)
+        loop(CW // OT, body)
 
     def dwo(p):
-        def body(t, _):
+        def body(t):
             cols = pl.ds(mul(t, OT), OT)
-            v = dot(jnp.concatenate([OA[p, s] for s in others], axis=0),
-                    jnp.concatenate([DYC[s, :, cols] for s in others], axis=0), 0, 0)
+            v = tn(jnp.concatenate([OA[p, s] for s in others], axis=0),
+                    jnp.concatenate([DYC[s, :, cols] for s in others], axis=0))
             dwo_ref[2 * p, :, cols] = dwo_ref[2 * p, :, cols] + v[:E]
             dwo_ref[2 * p + 1, :, cols] = dwo_ref[2 * p + 1, :, cols] + v[E:]
-            return 0
-        lax.fori_loop(0, CW // OT, body, 0)
+        loop(CW // OT, body)
 
     def dwq_own(p):
-        def body(t, _):
+        def body(t):
             cols = pl.ds(mul(t, OT), OT)
-            v = dot(XC[y, :, cols], DQA[p, y], 0, 0)
+            v = tn(XC[y, :, cols], DQA[p, y])
             dwq_ref[2 * p, cols, :] = v[:, :E]
             dwq_ref[2 * p + 1, cols, :] = v[:, E:]
-            return 0
-        lax.fori_loop(0, CW // OT, body, 0)
+        loop(CW // OT, body)
 
     def dwq(p):
-        def body(t, _):
+        def body(t):
             cols = pl.ds(mul(t, OT), OT)
-            v = dot(jnp.concatenate([XC[s, :, cols] for s in others], axis=0),
-                    jnp.concatenate([DQA[p, s] for s in others], axis=0), 0, 0)
+            v = tn(jnp.concatenate([XC[s, :, cols] for s in others], axis=0),
+                    jnp.concatenate([DQA[p, s] for s in others], axis=0))
             dwq_ref[2 * p, cols, :] = dwq_ref[2 * p, cols, :] + v[:, :E]
             dwq_ref[2 * p + 1, cols, :] = dwq_ref[2 * p + 1, cols, :] + v[:, E:]
-            return 0
-        lax.fori_loop(0, CW // OT, body, 0)
+        loop(CW // OT, body)
 
     def own_cols(dst, src):
-        def body(t, _):
+        def body(t):
             rows = pl.ds(pl.multiple_of(t * T, T), T)
             dst[y, rows, :] = src[y, rows, :]
-            return 0
-        lax.fori_loop(0, R // T, body, 0)
+        loop(R // T, body)
 
     own(0)
     own(1)
@@ -549,7 +548,7 @@
             far_fwd(1)
         if i == 1:
             far_fwd(0)
-        for n in range(i + 2, i + 3) if i < 5 else range(8, N_IT) if i == 7 else ():
+        for n in (i + 2,) if i < 5 else range(8, N_IT) if i == 7 else ():
             own(n)
         if i >= 1:
             opp(i - 1)
@@ -602,18 +601,18 @@
         yopp(p)
         dwo(p)
         if p == 1:
+            rs2(2)
             dwkv_mid()
-    rs2(2)
     for n in range(2):
         xc_fin(n)
     fin(N_IT - 1)
     yopp(NP)
     dwq(0)
+    rs2(3)
     dwkv_own()
     rs3(0)
     yopp(NP + 1)
     dwq(1)
-    rs2(3)
     rs3(1)
     yopp(NP + 2)
     dwq(2)

time: 120 us -> 120 us (level)
  no operation moved by 1% of the time
where the time goes in v6:
time: 120 us; the launch traced here: 119 us
  Pallas kernels  119 us (99%)
    pallas_call x1, Pallas kernels, device_step(): pl.pallas_call(functools.partial(kernel, cfg), out_shape=[V((T, D), BF16)...  114 us
    pallas_call x1, Pallas kernels, device_step(): pl.pallas_call(copy_out, out_shape=[jax.ShapeDtypeStruct(o.shape, o.dtype...  4.28 us

profile of v6, /device:TPU:97, one launch (start us, length us, event | category | flops | bytes accessed | tf_op | source)
XLA Modules:
  0.0 119.4 jit_solution(10953095307037681683)
XLA Ops:
  0.6 114.3 %attn_bwd_fused.1 = (bf16[64,6144]{1,0:T(8,128)(2,1)S(1)}, f32[6,1536,128]{2,1,0:T(8,128)S(1)}, f32[768,128]{1,0:T(8,128)S(1)}, f32[768,128]{1,0:T(8,128)S(1)}, f32[6,128,1536]{2,1,0:T(8,128)S(1)}) custom-call(bf16[64,6144]{1,0:T(8,128)(2,1)} %bitcast.6, bf16[64,6144]{1,0:T(8,128)(2,1)} %bitcast.7, bf16[6,6144,128]{2,1,0:T(8,128)(2,1)} %bitcast.5, ...), custom_call_target="tpu_custom_call" | custom-call | tf_op jit(solution)/shard_map/attn_bwd_fused/pallas_call | solution.py:683
  114.9 4.3 %write_results.1 = (bf16[64,6144]{1,0:T(8,128)(2,1)}, f32[6,1536,128]{2,1,0:T(8,128)}, f32[768,128]{1,0:T(8,128)}, f32[768,128]{1,0:T(8,128)}, f32[6,128,1536]{2,1,0:T(8,128)}) custom-call(bf16[64,6144]{1,0:T(8,128)(2,1)S(1)} %get-tuple-element.15.refs_0_, f32[6,1536,128]{2,1,0:T(8,128)S(1)} %get-tuple-element.16.refs_1_, ...), custom_call_target="tpu_custom_call" | custom-call | tf_op jit(solution)/shard_map/write_results/pallas_call | solution.py:693

commit v7 on v6

--- a/solution.py
+++ b/solution.py
@@ -12,6 +12,7 @@
 BF16 = jnp.bfloat16
 VMEM_BYTES = 55 * 1000 * 1000
 DXT = 384
+BY_Y = (8, 10)
 KTW = 768
 UNR = True
 OUT_IN = pl.ANY
@@ -43,7 +44,7 @@
            dx_ref, dwq_ref, dwk_ref, dwv_ref, dwo_ref,
            XS, DYS, XC, DYC, OA, DQA, QB, DOB, KV, KVACC, DKVR, DKVB,
            WQ, WKV, WO, MY, SX, KS, KR, ST,
-           agr, ags, a2ar, a2as, str_, sts, xcr, xcs, yr, ys, dkr, dks, pxr, pxs, rsr, rss, exs, exr,
+           agr, ags, a2ar, a2as, str_, sts, dcs, xcr, xcs, yr, ys, dkr, dks, pxr, pxs, rsr, rss, exs, exr,
            lx, ldy, lwq, lwkv, lwo, cred):
     T, CW, E, NX, NY, NH = cfg
     NP = NH // 2
@@ -132,6 +133,13 @@
             wait_recv(ST.at[t, n], str_.at[t, n])
             rc(ST.at[t, n], (DYC, XC)[t].at[seq((-1, 1)[n]), my_half(n)], sts.at[t, 2 + n], str_.at[t, 2 + n], dev).start()
 
+    def opp_half(n):
+        return pl.ds(pl.multiple_of(rb(2) + n * TH, TH), TH)
+
+    def dyc_send():
+        for n, dev in enumerate((YD, YU)):
+            rc(DYS.at[dy_order[2 - n], opp_half(n)], DYC.at[y, opp_half(n)], dcs.at[n], agr.at[BY_Y[n], 2 + n], dev).start()
+
     def own(i):
         buf, ix = items[i]
         if i >= 2 * NY:
@@ -151,12 +159,14 @@
         blk = buf.at[ix, pl.ds(lb, T)]
         wait_recv(blk, agr.at[i, 0])
         half = buf.at[ix, pl.ds(lb, TH)]
-        rc(half, half, ags.at[i], agr.at[i, 2], XR).start()
+        if i != BY_Y[0]:
+            rc(half, half, ags.at[i], agr.at[i, 2], XR).start()
         rc(blk, blk, ags.at[i], agr.at[i, 4], PT).start()
         blk = buf.at[ix, pl.ds(rb_, T)]
         wait_recv(blk, agr.at[i, 1])
         half = buf.at[ix, pl.ds(pl.multiple_of(rb_ + TH, TH), TH)]
-        rc(half, half, ags.at[i], agr.at[i, 3], XL).start()
+        if i != BY_Y[1]:
+            rc(half, half, ags.at[i], agr.at[i, 3], XL).start()
         rc(blk, blk, ags.at[i], agr.at[i, 4], PT).start()
 
     def opp(i):
@@ -173,7 +183,7 @@
 
     def ag_sent(i):
         buf, ix = items[i]
-        wait_send(buf.at[ix, pl.ds(0, 7 * T)], ags.at[i])
+        wait_send(buf.at[ix, pl.ds(0, 7 * T - (TH if i in BY_Y else 0))], ags.at[i])
 
     par = pl.ds(mul(h, HR), HR)
 
@@ -516,11 +526,11 @@
                 KV[0] = KVACC[:, :E].astype(BF16)
                 KV[1] = KVACC[:, E:].astype(BF16)
                 for p in range(NP):
+                    if p < 2:
+                        fwd(NY + p)
+                        own(NY + p + 2)
                     attn_fwd(p)
                     yown(p)
-                    if p == 0:
-                        fwd(5)
-                        own(7)
                 own_cols(XC, XS)
         elif i < 8:
             proj_dy(i - NY)
@@ -532,6 +542,7 @@
                 dwo_own(0)
                 dwo_own(1)
             if i == 6:
+                dyc_send()
                 xc_fwd(1)
                 yfwd(1)
                 dwo_own(2)
@@ -542,13 +553,13 @@
                 KVACC[...] = jnp.zeros_like(KVACC)
 
     for i in range(9):
-        if i < 8 and i != 5:
+        if i not in (4, 5, 8):
             fwd(i)
         if i == 0:
             far_fwd(1)
         if i == 1:
             far_fwd(0)
-        for n in (i + 2,) if i < 5 else range(8, N_IT) if i == 7 else ():
+        for n in (4, 5) if i == 3 else () if i == 2 else (i + 2,) if i < 4 else range(8, N_IT) if i == 7 else ():
             own(n)
         if i >= 1:
             opp(i - 1)
@@ -568,19 +579,20 @@
     wait_send(DYS.at[0, pl.ds(0, 2 * T)], a2as.at[0])
     for n in range(2):
         wait_send(DYS.at[0, pl.ds(0, TH)], sts.at[0, n])
+        wait_send(DYS.at[0, pl.ds(0, TH)], dcs.at[n])
     dkv_send()
     for p in range(NP):
         dwq_own(p)
     fwd(10)
     dkv_sum()
     dxc(0)
-    yfwd(NP)
     dxc(1)
     fwd(11)
     pl.semaphore_wait(cred, 2)
     rs1(0)
     opp(8)
     dwkv_early()
+    yfwd(NP)
     dxc(2)
     rs1(1)
     yfwd(NP + 1)
@@ -675,7 +687,7 @@
             V((NH, CW, E), BF16), V((2, CW, E), BF16), V((NH, E, CW), BF16),
             V((NY, R // 2, CW), F32), V((NY, 3 * T, CW), BF16), V((NY - 1, KB, 2 * E), BF16), V((NY - 1, KB, 2 * E), BF16),
             V((2, 2, T // 2, CW), BF16),
-            S((n_it, 5)), S((n_it,)), S((NY,)), S((1,)), S((2, 4)), S((2, 4)), S((4,)), S((4,)), S((2 * NP, 4)), S((2 * NP,)),
+            S((n_it, 5)), S((n_it,)), S((NY,)), S((1,)), S((2, 4)), S((2, 4)), S((2,)), S((4,)), S((4,)), S((2 * NP, 4)), S((2 * NP,)),
             S((4,)), S((3,)), S((NY,)), S((NY,)), S((NY, 4)), S((NY,)), S((1,)), S((1,)),
             S((NY,)), S((NY,)), S((3,)), S((6,)), S((1,)), pltpu.SemaphoreType.REGULAR,
         ]

time: 120 us -> 119 us (level)
  no operation moved by 1% of the time
where the time goes in v7:
time: 119 us
  Pallas kernels  118 us (99%)
    pallas_call x1, Pallas kernels, device_step(): pl.pallas_call(functools.partial(kernel, cfg), out_shape=[V((T, D), BF16)...  114 us
    pallas_call x1, Pallas kernels, device_step(): pl.pallas_call(copy_out, out_shape=[jax.ShapeDtypeStruct(o.shape, o.dtype...  4.28 us

profile of v7, /device:TPU:97, one launch (start us, length us, event | category | flops | bytes accessed | tf_op | source)
XLA Modules:
  0.0 118.7 jit_solution(954889405518881308)
XLA Ops:
  0.6 113.6 %attn_bwd_fused.1 = (bf16[64,6144]{1,0:T(8,128)(2,1)S(1)}, f32[6,1536,128]{2,1,0:T(8,128)S(1)}, f32[768,128]{1,0:T(8,128)S(1)}, f32[768,128]{1,0:T(8,128)S(1)}, f32[6,128,1536]{2,1,0:T(8,128)S(1)}) custom-call(bf16[64,6144]{1,0:T(8,128)(2,1)} %bitcast.6, bf16[64,6144]{1,0:T(8,128)(2,1)} %bitcast.7, bf16[6,6144,128]{2,1,0:T(8,128)(2,1)} %bitcast.5, ...), custom_call_target="tpu_custom_call" | custom-call | tf_op jit(solution)/shard_map/attn_bwd_fused/pallas_call | solution.py:695
  114.3 4.3 %write_results.1 = (bf16[64,6144]{1,0:T(8,128)(2,1)}, f32[6,1536,128]{2,1,0:T(8,128)}, f32[768,128]{1,0:T(8,128)}, f32[768,128]{1,0:T(8,128)}, f32[6,128,1536]{2,1,0:T(8,128)}) custom-call(bf16[64,6144]{1,0:T(8,128)(2,1)S(1)} %get-tuple-element.15.refs_0_, f32[6,1536,128]{2,1,0:T(8,128)S(1)} %get-tuple-element.16.refs_1_, ...), custom_call_target="tpu_custom_call" | custom-call | tf_op jit(solution)/shard_map/write_results/pallas_call | solution.py:705

commit v8 on v7

--- a/solution.py
+++ b/solution.py
@@ -51,6 +51,7 @@
     R = 2 * NX * T
     HR = NX * T
     TH = T // 2
+    TQ = T // 4
     scale = E ** -0.5
     scale2 = scale * LOG2E
     pod = lax.axis_index('pod')
@@ -134,7 +135,7 @@
             rc(ST.at[t, n], (DYC, XC)[t].at[seq((-1, 1)[n]), my_half(n)], sts.at[t, 2 + n], str_.at[t, 2 + n], dev).start()
 
     def opp_half(n):
-        return pl.ds(pl.multiple_of(rb(2) + n * TH, TH), TH)
+        return pl.ds(pl.multiple_of(rb(2) + n * TH + TQ, TQ), TQ)
 
     def dyc_send():
         for n, dev in enumerate((YD, YU)):
@@ -158,15 +159,13 @@
         lb, rb_ = rb(-1), rb(1)
         blk = buf.at[ix, pl.ds(lb, T)]
         wait_recv(blk, agr.at[i, 0])
-        half = buf.at[ix, pl.ds(lb, TH)]
-        if i != BY_Y[0]:
-            rc(half, half, ags.at[i], agr.at[i, 2], XR).start()
+        half = buf.at[ix, pl.ds(lb, TQ if i == BY_Y[0] else TH)]
+        rc(half, half, ags.at[i], agr.at[i, 2], XR).start()
         rc(blk, blk, ags.at[i], agr.at[i, 4], PT).start()
         blk = buf.at[ix, pl.ds(rb_, T)]
         wait_recv(blk, agr.at[i, 1])
-        half = buf.at[ix, pl.ds(pl.multiple_of(rb_ + TH, TH), TH)]
-        if i != BY_Y[1]:
-            rc(half, half, ags.at[i], agr.at[i, 3], XL).start()
+        half = buf.at[ix, pl.ds(pl.multiple_of(rb_ + TH, TH), TQ if i == BY_Y[1] else TH)]
+        rc(half, half, ags.at[i], agr.at[i, 3], XL).start()
         rc(blk, blk, ags.at[i], agr.at[i, 4], PT).start()
 
     def opp(i):
@@ -183,7 +182,7 @@
 
     def ag_sent(i):
         buf, ix = items[i]
-        wait_send(buf.at[ix, pl.ds(0, 7 * T - (TH if i in BY_Y else 0))], ags.at[i])
+        wait_send(buf.at[ix, pl.ds(0, 7 * T - (TQ if i in BY_Y else 0))], ags.at[i])
 
     par = pl.ds(mul(h, HR), HR)
 
@@ -579,7 +578,7 @@
     wait_send(DYS.at[0, pl.ds(0, 2 * T)], a2as.at[0])
     for n in range(2):
         wait_send(DYS.at[0, pl.ds(0, TH)], sts.at[0, n])
-        wait_send(DYS.at[0, pl.ds(0, TH)], dcs.at[n])
+        wait_send(DYS.at[0, pl.ds(0, TQ)], dcs.at[n])
     dkv_send()
     for p in range(NP):
         dwq_own(p)

time: 119 us -> 119 us (level)
  no operation moved by 1% of the time
where the time goes in v8:
time: 119 us
  Pallas kernels  118 us (99%)
    pallas_call x1, Pallas kernels, device_step(): pl.pallas_call(functools.partial(kernel, cfg), out_shape=[V((T, D), BF16)...  114 us
    pallas_call x1, Pallas kernels, device_step(): pl.pallas_call(copy_out, out_shape=[jax.ShapeDtypeStruct(o.shape, o.dtype...  4.28 us

profile of v8, /device:TPU:97, one launch (start us, length us, event | category | flops | bytes accessed | tf_op | source)
XLA Modules:
  0.0 119.0 jit_solution(8403512532929230319)
XLA Ops:
  0.6 113.9 %attn_bwd_fused.1 = (bf16[64,6144]{1,0:T(8,128)(2,1)S(1)}, f32[6,1536,128]{2,1,0:T(8,128)S(1)}, f32[768,128]{1,0:T(8,128)S(1)}, f32[768,128]{1,0:T(8,128)S(1)}, f32[6,128,1536]{2,1,0:T(8,128)S(1)}) custom-call(bf16[64,6144]{1,0:T(8,128)(2,1)} %bitcast.6, bf16[64,6144]{1,0:T(8,128)(2,1)} %bitcast.7, bf16[6,6144,128]{2,1,0:T(8,128)(2,1)} %bitcast.5, ...), custom_call_target="tpu_custom_call" | custom-call | tf_op jit(solution)/shard_map/attn_bwd_fused/pallas_call | solution.py:694
  114.5 4.3 %write_results.1 = (bf16[64,6144]{1,0:T(8,128)(2,1)}, f32[6,1536,128]{2,1,0:T(8,128)}, f32[768,128]{1,0:T(8,128)}, f32[768,128]{1,0:T(8,128)}, f32[6,128,1536]{2,1,0:T(8,128)}) custom-call(bf16[64,6144]{1,0:T(8,128)(2,1)S(1)} %get-tuple-element.15.refs_0_, f32[6,1536,128]{2,1,0:T(8,128)S(1)} %get-tuple-element.16.refs_1_, ...), custom_call_target="tpu_custom_call" | custom-call | tf_op jit(solution)/shard_map/write_results/pallas_call | solution.py:704
